TPU v7x, 512 devices: a whole 4x8x8 slice. The times are simulated.
512 devices in a mesh: gx: 8 (over z), gy: 4 (over x_lo, core), gz: 16 (over y, x_hi).
Axes of the slice: x: 4 (x_hi: 2, x_lo: 2; x = x_hi * 2 + x_lo), y: 8, z: 8, core: 2. Of those that a mesh axis runs over, the one named last changes fastest.
Arguments:
- probe_bits: int32 [32, 128, 512], P('gx', 'gz', 'gy'), may hold values from -2147483648 to 2147483646
- disorder_levels: int32 [32, 128, 512], P('gx', 'gz', 'gy'), may hold values from -2147483648 to 2147483647, as said below
Outputs:
- moments: float32 [3, 8], replicated
- previous: float32 [8, 32, 512, 512], P(None, 'gx', 'gz', 'gy')
- current: float32 [8, 32, 512, 512], P(None, 'gx', 'gz', 'gy')
Inputs may be any that keep to these rules, and one draw needn't show every extreme that they name: `disorder_levels`: every byte of a word is a level 0 to 255.
All inputs are finite; a program needn't handle non-finite values.
Results may differ from a plain program's by a relative error of at most 0.00002.
Values sent between devices are 32-bit elements; how exact they have to be, the bound alone decides.
A program may use at most 64 MiB of HBM per device.

v0:
```python
import functools

import jax
import jax.numpy as jnp
from jax import lax
from jax.sharding import Mesh
from jax.sharding import PartitionSpec as P

PROBES = 8
LEVELS = 256
GX_GY_GZ = ("gx", "gy_0", "gy_1", "gz_0", "gz_1")
GY = ("gy_0", "gy_1")
GZ = ("gz_0", "gz_1")


disorder_width = 4.0
spectral_scale = 8.4


def with_halo(cells, sides, width):
    for axis, dim in sides:
        count = lax.axis_size(axis)
        head = lax.slice_in_dim(cells, 0, width, axis=dim)
        tail = lax.slice_in_dim(cells, cells.shape[dim] - width, cells.shape[dim], axis=dim)
        cells = jnp.concatenate(
            [
                lax.ppermute(tail, axis, [(i, (i + 1) % count) for i in range(count)]),
                cells,
                lax.ppermute(head, axis, [((i + 1) % count, i) for i in range(count)]),
            ],
            axis=dim,
        )
    return cells


def by_axis(array, axes):
    return functools.reduce(lax.psum, axes, array)


def unpack_signs(packed):
    shifts = (
        4 * jnp.arange(PROBES, dtype=jnp.int32)[:, None] + jnp.arange(4, dtype=jnp.int32)[None, :]
    )
    bit_values = jnp.right_shift(packed[None, :, :, None, :], shifts[:, None, None, :, None]) & 1
    layout = bit_values.shape
    flat = bit_values.reshape(layout[0], layout[1], layout[2] * layout[3], layout[4])
    return 2.0 * flat.astype(jnp.float32) - 1.0


def unpack_energy(packed):
    shifts = 8 * jnp.arange(4, dtype=jnp.int32)
    levels = jnp.right_shift(packed[:, :, None, :], shifts[None, None, :, None]) & 255
    layout = levels.shape
    flat = levels.reshape(layout[0], layout[1] * layout[2], layout[3])
    return disorder_width * ((flat.astype(jnp.float32) + 0.5) / LEVELS - 0.5)


def crop_sites(block, margin):
    return block[..., margin:-margin, margin:-margin, margin:-margin]


def crop_depth(block, margin):
    return block[..., margin:-margin, :]


def valid_ham(padded, energy):
    center = padded[:, 1:-1, 1:-1, 1:-1]
    beside = padded[:, 2:, 1:-1, 1:-1] + padded[:, :-2, 1:-1, 1:-1]
    beside = beside + padded[:, 1:-1, 1:-1, 2:] + padded[:, 1:-1, 1:-1, :-2]
    beside = beside + padded[:, 1:-1, 2:, 1:-1] + padded[:, 1:-1, :-2, 1:-1]
    return (energy[None] * center - beside) / spectral_scale


def per_device(probe_bits, disorder_levels):
    stacked = jnp.stack([probe_bits, disorder_levels], 0)
    extended = with_halo(stacked, (("gx", 1), (GY, 3), (GZ, 2)), 3)
    signs_wide = crop_depth(unpack_signs(extended[0]), 9)
    energy_wide = crop_depth(unpack_energy(extended[1]), 9)
    first_wide = valid_ham(signs_wide, crop_sites(energy_wide, 1))
    second_wide = 2.0 * valid_ham(first_wide, crop_sites(energy_wide, 2)) - crop_sites(
        signs_wide, 2
    )
    third = 2.0 * valid_ham(second_wide, crop_sites(energy_wide, 3)) - crop_sites(first_wide, 2)
    signs = crop_sites(signs_wide, 3)
    first = crop_sites(first_wide, 2)
    second = crop_sites(second_wide, 1)
    partial_sums = [jnp.sum(signs * vec, axis=(1, 2, 3)) for vec in (first, second, third)]
    total_sites = (
        third.shape[1]
        * third.shape[2]
        * third.shape[3]
        * lax.axis_size("gx")
        * lax.axis_size(GY)
        * lax.axis_size(GZ)
    )
    summed = [by_axis(part_sum, GX_GY_GZ) for part_sum in partial_sums]
    moments = jnp.stack(summed) / total_sites
    return (moments, second, third)


def solution(mesh):
    torus = Mesh(
        mesh.devices.reshape(mesh.shape["gx"], 2, 2, 8, 2), ("gx", "gy_0", "gy_1", "gz_0", "gz_1")
    )
    return jax.shard_map(
        per_device,
        mesh=torus,
        in_specs=(P("gx", GZ, GY), P("gx", GZ, GY)),
        out_specs=(P(), P(None, "gx", GZ, GY), P(None, "gx", GZ, GY)),
        check_vma=False,
    )
```

profile of v0, /device:TPU:6, one launch (start us, length us, event | category | flops | bytes accessed | tf_op | source)
XLA Modules:
  0.0 101.9 jit_solution(648168939208347832)
XLA Ops:
  0.6 0.8 fusion.7
  1.4 4.3 %collective-permute-start = (s32[2,3,8,128]{3,2,1,0:T(8,128)S(1)}, s32[2,3,8,128]{3,2,1,0:T(8,128)S(1)}, u32[]{:S(2)}, u32[]{:S(2)}) collective-permute-start(s32[2,3,8,128]{3,2,1,0:T(8,128)S(1)} %get-tuple-element.29), channel_id=1, source_target_pairs={{0,64},{64,128},{128,192},{192,256},{256,320},{320,384},{384,448},... | collective-permute-start | bytes 73736 | tf_op jit(solution)/shard_map/ppermute | solution.py:27
  5.7 8.6 %collective-permute-start.1 = (s32[2,3,8,128]{3,2,1,0:T(8,128)S(1)}, s32[2,3,8,128]{3,2,1,0:T(8,128)S(1)}, u32[]{:S(2)}, u32[]{:S(2)}) collective-permute-start(s32[2,3,8,128]{3,2,1,0:T(8,128)S(1)} %get-tuple-element.30), channel_id=1, source_target_pairs={{64,0},{128,64},{192,128},{256,192},{320,256},{384,320},{448,384},... | collective-permute-start | bytes 73736 | tf_op jit(solution)/shard_map/ppermute | solution.py:29
  14.3 0.0 collective-permute-done
  14.3 1.5 %collective-permute-done.1 = s32[2,3,8,128]{3,2,1,0:T(8,128)S(1)} collective-permute-done((s32[2,3,8,128]{3,2,1,0:T(8,128)S(1)}, s32[2,3,8,128]{3,2,1,0:T(8,128)S(1)}, u32[]{:S(2)}, u32[]{:S(2)}) %collective-permute-start.1) | collective-permute-done | bytes 24608 | tf_op jit(solution)/shard_map/ppermute | solution.py:29
  15.8 0.7 pad_add_fusion.2
  16.5 0.1 fusion.10
  16.6 1.9 %collective-permute-start.2 = (s32[2,10,8,3]{3,2,1,0:T(8,128)S(1)}, s32[2,10,8,3]{3,2,1,0:T(8,128)S(1)}, u32[]{:S(2)}, u32[]{:S(2)}) collective-permute-start(s32[2,10,8,3]{3,2,1,0:T(8,128)S(1)} %get-tuple-element.27), channel_id=1, source_target_pairs={{0,16},{16,32},{32,48},{48,0},{1,17},{17,33},{33,49},{49,1},{2,18}... | collective-permute-start | bytes 5768 | tf_op jit(solution)/shard_map/ppermute | solution.py:27
  18.5 3.6 %collective-permute-start.3 = (s32[2,10,8,3]{3,2,1,0:T(8,128)S(1)}, s32[2,10,8,3]{3,2,1,0:T(8,128)S(1)}, u32[]{:S(2)}, u32[]{:S(2)}) collective-permute-start(s32[2,10,8,3]{3,2,1,0:T(8,128)S(1)} %get-tuple-element.28), channel_id=1, source_target_pairs={{16,0},{32,16},{48,32},{0,48},{17,1},{33,17},{49,33},{1,49},{18,2}... | collective-permute-start | bytes 5768 | tf_op jit(solution)/shard_map/ppermute | solution.py:29
  22.2 0.2 collective-permute-done.2
  22.4 1.9 %collective-permute-done.3 = s32[2,10,8,3]{3,2,1,0:T(8,128)S(1)} collective-permute-done((s32[2,10,8,3]{3,2,1,0:T(8,128)S(1)}, s32[2,10,8,3]{3,2,1,0:T(8,128)S(1)}, u32[]{:S(2)}, u32[]{:S(2)}) %collective-permute-start.3) | collective-permute-done | bytes 1952 | tf_op jit(solution)/shard_map/ppermute | solution.py:29
  24.2 0.9 pad_add_fusion.1
  25.1 4.3 %collective-permute-start.4 = (s32[2,10,3,134]{3,2,1,0:T(4,128)S(1)}, s32[2,10,3,134]{3,2,1,0:T(4,128)S(1)}, u32[]{:S(2)}, u32[]{:S(2)}) collective-permute-start(s32[2,10,3,134]{3,2,1,0:T(4,128)S(1)} %get-tuple-element.25), channel_id=1, source_target_pairs={{0,1},{1,2},{2,3},{3,4},{4,5},{5,6},{6,7},{7,8},{8,9},{9,10},{10,1... | collective-permute-start | bytes 96488 | tf_op jit(solution)/shard_map/ppermute | solution.py:27
  29.5 3.0 %collective-permute-start.5 = (s32[2,10,3,134]{3,2,1,0:T(4,128)S(1)}, s32[2,10,3,134]{3,2,1,0:T(4,128)S(1)}, u32[]{:S(2)}, u32[]{:S(2)}) collective-permute-start(s32[2,10,3,134]{3,2,1,0:T(4,128)S(1)} %get-tuple-element.26), channel_id=1, source_target_pairs={{1,0},{2,1},{3,2},{4,3},{5,4},{6,5},{7,6},{8,7},{9,8},{10,9},{11,1... | collective-permute-start | bytes 96488 | tf_op jit(solution)/shard_map/ppermute | solution.py:29
  32.5 0.1 shift_right_arithmetic.58
  32.6 0.1 copy.5
  32.7 1.1 %collective-permute-done.4 = s32[2,10,3,134]{3,2,1,0:T(4,128)S(1)} collective-permute-done((s32[2,10,3,134]{3,2,1,0:T(4,128)S(1)}, s32[2,10,3,134]{3,2,1,0:T(4,128)S(1)}, u32[]{:S(2)}, u32[]{:S(2)}) %collective-permute-start.4) | collective-permute-done | bytes 32192 | tf_op jit(solution)/shard_map/ppermute | solution.py:27
  33.8 4.7 %collective-permute-done.5 = s32[2,10,3,134]{3,2,1,0:T(4,128)S(1)} collective-permute-done((s32[2,10,3,134]{3,2,1,0:T(4,128)S(1)}, s32[2,10,3,134]{3,2,1,0:T(4,128)S(1)}, u32[]{:S(2)}, u32[]{:S(2)}) %collective-permute-start.5) | collective-permute-done | bytes 32192 | tf_op jit(solution)/shard_map/ppermute | solution.py:29
  38.6 0.9 pad_add_fusion
  39.5 0.1 shift_right_arithmetic.55
  39.6 0.2 shift_right_arithmetic.56
  39.8 0.2 add_multiply_fusion
  40.0 0.1 slice.184
  40.1 0.1 slice.174
  40.3 0.2 slice.165
  40.4 0.1 shift_right_arithmetic.47
  40.5 0.2 shift_right_arithmetic.48
  40.7 0.8 multiply_add_fusion
  41.5 4.5 %fusion.1 = f32[8,8,36,132]{3,2,1,0:T(8,128)S(1)} fusion(f32[8,10,56,134]{3,2,1,0:T(8,128)S(1)} %multiply_add_fusion, f32[8,36,132]{2,1,0:T(8,128)S(1)} %slice.165), kind=kLoop, calls=%fused_computation.3 | loop fusion | flops 2433024 | bytes 9884160 | tf_op jit(solution)/shard_map/div | solution.py:71
  46.1 3.6 %slice_subtract_fusion = f32[8,6,34,130]{3,2,1,0:T(8,128)S(1)} fusion(f32[8,10,56,134]{3,2,1,0:T(8,128)S(1)} %multiply_add_fusion, f32[8,8,36,132]{3,2,1,0:T(8,128)S(1)} %fusion.1, f32[6,34,130]{2,1,0:T(8,128)S(1)} %slice.174), kind=kLoop, calls=%fused_computation.9 | loop fusion | flops 1909440 | bytes 7743840 | tf_op jit(solution)/shard_map/sub | solution.py:80
  49.7 2.1 %multiply_reduce_fusion.2 = (f32[8]{0:T(128)S(1)}, f32[8]{0:T(128)S(1)}, f32[8]{0:T(128)S(1)}, f32[8,4,32,128]{3,2,1,0:T(8,128)}, f32[8,4,32,128]{3,2,1,0:T(8,128)}) fusion(f32[8,8,36,132]{3,2,1,0:T(8,128)S(1)} %fusion.1, f32[8,10,56,134]{3,2,1,0:T(8,128)S(1)} %multiply_add_fusion, f32[8,6,34,130]{3,2,1,0:T(8,128)S(1)} %slice_subtract_fusion, ...), kind=kLoop, calls=%fused_computation.29 | loop fusion | flops 1966056 | bytes 5832800 | tf_op jit(solution)/shard_map/reduce_sum | solution.py:87
  51.9 17.6 %all-reduce.1 = (f32[8]{0:T(128)S(1)}, f32[8]{0:T(128)S(1)}, f32[8]{0:T(128)S(1)}) all-reduce(f32[8]{0:T(128)S(1)} %get-tuple-element.5, f32[8]{0:T(128)S(1)} %get-tuple-element.4, f32[8]{0:T(128)S(1)} %get-tuple-element.3), channel_id=1, replica_groups=mesh['gx'=8,'gy_0'=2,'gy_1'=2,'gz_0'=8,'gz_1'=2] {'gx'}, use_global_device_ids=true, to_apply=%region_13.0 | all-reduce | flops 24 | bytes 192 | tf_op jit(solution)/shard_map/psum | solution.py:37
  69.5 4.9 %all-reduce.4 = (f32[8]{0:T(128)S(1)}, f32[8]{0:T(128)S(1)}, f32[8]{0:T(128)S(1)}) all-reduce(f32[8]{0:T(128)S(1)} %get-tuple-element.9, f32[8]{0:T(128)S(1)} %get-tuple-element.10, f32[8]{0:T(128)S(1)} %get-tuple-element.11), channel_id=1, replica_groups=mesh['gx'=8,'gy_0'=2,'gy_1'=2,'gz_0'=8,'gz_1'=2] {'gy_0'}, use_global_device_ids=true, to_apply=%region_14.0 | all-reduce | flops 24 | bytes 192 | tf_op jit(solution)/shard_map/psum | solution.py:37
  74.4 2.4 %all-reduce.3 = (f32[8]{0:T(128)S(1)}, f32[8]{0:T(128)S(1)}, f32[8]{0:T(128)S(1)}) all-reduce(f32[8]{0:T(128)S(1)} %get-tuple-element.18, f32[8]{0:T(128)S(1)} %get-tuple-element.19, f32[8]{0:T(128)S(1)} %get-tuple-element.20), channel_id=1, replica_groups=mesh['gx'=8,'gy_0'=2,'gy_1'=2,'gz_0'=8,'gz_1'=2] {'gy_1'}, use_global_device_ids=true, to_apply=%region_15.0 | all-reduce | flops 24 | bytes 192 | tf_op jit(solution)/shard_map/psum | solution.py:37
  76.9 18.0 %all-reduce = (f32[8]{0:T(128)S(1)}, f32[8]{0:T(128)S(1)}, f32[8]{0:T(128)S(1)}) all-reduce(f32[8]{0:T(128)S(1)} %get-tuple-element.15, f32[8]{0:T(128)S(1)} %get-tuple-element.16, f32[8]{0:T(128)S(1)} %get-tuple-element.17), channel_id=1, replica_groups=mesh['gx'=8,'gy_0'=2,'gy_1'=2,'gz_0'=8,'gz_1'=2] {'gz_0'}, use_global_device_ids=true, to_apply=%region_16.0 | all-reduce | flops 24 | bytes 192 | tf_op jit(solution)/shard_map/psum | solution.py:37
  94.9 6.4 %all-reduce.2 = (f32[1,8]{1,0:T(1,128)S(1)}, f32[1,8]{1,0:T(1,128)S(1)}, f32[1,8]{1,0:T(1,128)S(1)}) all-reduce(f32[1,8]{1,0:T(1,128)S(1)} %bitcast.19, f32[1,8]{1,0:T(1,128)S(1)} %bitcast.20, f32[1,8]{1,0:T(1,128)S(1)} %bitcast.21), channel_id=1, replica_groups=mesh['gx'=8,'gy_0'=2,'gy_1'=2,'gz_0'=8,'gz_1'=2] {'gz_1'}, use_global_device_ids=true, to_apply=%region_17.0 | all-reduce | flops 24 | bytes 192 | tf_op jit(solution)/shard_map/psum | solution.py:37
  101.4 0.6 maximum_multiply_fusion
  (7 shorter events, 0.1 us)
Async XLA Ops:
  1.4 12.9 %collective-permute-start = (s32[2,3,8,128]{3,2,1,0:T(8,128)S(1)}, s32[2,3,8,128]{3,2,1,0:T(8,128)S(1)}, u32[]{:S(2)}, u32[]{:S(2)}) collective-permute-start(s32[2,3,8,128]{3,2,1,0:T(8,128)S(1)} %get-tuple-element.29), channel_id=1, source_target_pairs={{0,64},{64,128},{128,192},{192,256},{256,320},{320,384},{384,448},... | collective-permute-start | bytes 73736 | tf_op jit(solution)/shard_map/ppermute | solution.py:27
  5.7 10.1 %collective-permute-start.1 = (s32[2,3,8,128]{3,2,1,0:T(8,128)S(1)}, s32[2,3,8,128]{3,2,1,0:T(8,128)S(1)}, u32[]{:S(2)}, u32[]{:S(2)}) collective-permute-start(s32[2,3,8,128]{3,2,1,0:T(8,128)S(1)} %get-tuple-element.30), channel_id=1, source_target_pairs={{64,0},{128,64},{192,128},{256,192},{320,256},{384,320},{448,384},... | collective-permute-start | bytes 73736 | tf_op jit(solution)/shard_map/ppermute | solution.py:29
  16.6 5.8 %collective-permute-start.2 = (s32[2,10,8,3]{3,2,1,0:T(8,128)S(1)}, s32[2,10,8,3]{3,2,1,0:T(8,128)S(1)}, u32[]{:S(2)}, u32[]{:S(2)}) collective-permute-start(s32[2,10,8,3]{3,2,1,0:T(8,128)S(1)} %get-tuple-element.27), channel_id=1, source_target_pairs={{0,16},{16,32},{32,48},{48,0},{1,17},{17,33},{33,49},{49,1},{2,18}... | collective-permute-start | bytes 5768 | tf_op jit(solution)/shard_map/ppermute | solution.py:27
  18.5 5.7 %collective-permute-start.3 = (s32[2,10,8,3]{3,2,1,0:T(8,128)S(1)}, s32[2,10,8,3]{3,2,1,0:T(8,128)S(1)}, u32[]{:S(2)}, u32[]{:S(2)}) collective-permute-start(s32[2,10,8,3]{3,2,1,0:T(8,128)S(1)} %get-tuple-element.28), channel_id=1, source_target_pairs={{16,0},{32,16},{48,32},{0,48},{17,1},{33,17},{49,33},{1,49},{18,2}... | collective-permute-start | bytes 5768 | tf_op jit(solution)/shard_map/ppermute | solution.py:29
  25.1 8.7 %collective-permute-start.4 = (s32[2,10,3,134]{3,2,1,0:T(4,128)S(1)}, s32[2,10,3,134]{3,2,1,0:T(4,128)S(1)}, u32[]{:S(2)}, u32[]{:S(2)}) collective-permute-start(s32[2,10,3,134]{3,2,1,0:T(4,128)S(1)} %get-tuple-element.25), channel_id=1, source_target_pairs={{0,1},{1,2},{2,3},{3,4},{4,5},{5,6},{6,7},{7,8},{8,9},{9,10},{10,1... | collective-permute-start | bytes 96488 | tf_op jit(solution)/shard_map/ppermute | solution.py:27
  29.5 9.1 %collective-permute-start.5 = (s32[2,10,3,134]{3,2,1,0:T(4,128)S(1)}, s32[2,10,3,134]{3,2,1,0:T(4,128)S(1)}, u32[]{:S(2)}, u32[]{:S(2)}) collective-permute-start(s32[2,10,3,134]{3,2,1,0:T(4,128)S(1)} %get-tuple-element.26), channel_id=1, source_target_pairs={{1,0},{2,1},{3,2},{4,3},{5,4},{6,5},{7,6},{8,7},{9,8},{10,9},{11,1... | collective-permute-start | bytes 96488 | tf_op jit(solution)/shard_map/ppermute | solution.py:29
where the time goes:
time: 103 us; the launch traced here: 102 us
  blocking collectives  49.5 us (48%)
  starting transfers between devices  25.8 us (25%)
  other arithmetic  15.2 us (15%)
  waiting for transfers between devices  9.37 us (9%)
  local copies, waits for them, and re-layouts  1.25 us (1%)
    psum x5, blocking collectives, by_axis(): return functools.reduce(lax.psum, axes, array)  49.5 us
    ppermute x3, starting transfers between devices, with_halo(): lax.ppermute(head, axis, [((i + 1) % count, i) for i in range(count)])  15.2 us
    ppermute x3, starting transfers between devices, with_halo(): lax.ppermute(tail, axis, [(i, (i + 1) % count) for i in range(count)])  10.5 us
    ppermute x3, waiting for transfers between devices, with_halo(): lax.ppermute(head, axis, [((i + 1) % count, i) for i in range(count)])  8.07 us
    div x1, other arithmetic, valid_ham(): return (energy[None] * center - beside) / spectral_scale  4.54 us
    sub x1, other arithmetic, per_device(): 2.0 * valid_ham(first_wide, crop_sites(energy_wide, 2))  3.64 us
    concatenate x3, other arithmetic, with_halo(): jnp.concatenate([lax.ppermute(tail, axis, [(i, (i + 1) % count) for i in...  2.53 us
    reduce_sum x1, other arithmetic, per_device(): jnp.sum(signs * vec, axis=(1, 2, 3))  2.12 us
  transfers between devices with their start and end apart: 6, of which 5 were waited for; matrix products, arithmetic and copies ran while one was open for 0% of the time, Pallas kernels for 0%

commit v1 on v0

v1 whole, which is shorter than its diff:
```python
import jax
import jax.numpy as jnp
from jax import lax
from jax.experimental import pallas as pl
from jax.experimental.pallas import tpu as pltpu
from jax.sharding import PartitionSpec as P

F32 = jnp.float32
I32 = jnp.int32
MESH = pl.DeviceIdType.MESH
C1 = 1.0 / 8.4
C2 = 2.0 / 8.4
SIZES = {"gx": 8, "gy": 4, "gz": 16}
NSITES = 32 * 512 * 512
LOCAL = 4 * 32 * 128

DIRS = sorted(
    [
        (dx, dy, dz)
        for dx in (-1, 0, 1)
        for dy in (-1, 0, 1)
        for dz in (-1, 0, 1)
        if (dx, dy, dz) != (0, 0, 0)
    ],
    key=lambda d: (-abs(d[2]), abs(d[0]) + abs(d[1])),
)


def srl(a, n):
    return lax.shift_right_logical(a, n if hasattr(n, "shape") and n.shape == a.shape else jnp.full(a.shape, n, I32))


def roll(a, n, axis):
    return pltpu.roll(a, n % a.shape[axis], axis)


def count_bits(a, b, c, d, e, f):
    x = a ^ b
    s1 = x ^ c
    c1 = (a & b) | (c & x)
    y = d ^ e
    s2 = y ^ f
    c2 = (d & e) | (f & y)
    h = s1 & s2
    z = c1 ^ c2
    return s1 ^ s2, z ^ h, (c1 & c2) | (h & z)


def nibbles(planes, word, shift):
    ones = 0x11111111
    p0, p1, p2 = planes
    return (
        (srl(p0, shift) & ones)
        | ((srl(p1, shift) & ones) << 1)
        | ((srl(p2, shift) & ones) << 2)
        | ((srl(word, shift) & ones) << 3)
    )


def kernel(
    bits_hbm, dis_hbm, mom, prev, cur,
    E, NM, NZ1, NZ2, NY, NY2,
    EPM, EMM, E2M, EPZ1, EMZ1, EPZ2, EMZ2, E2Z, EPY, EMY, E2Y, EPY2, EMY2,
    V1M, V1Z1, V1Z2, V1Y, V1YI, V1Y2I, V1Y2, V2M, V2Z, V2YI, ACC, S, G,
    in_sem, hs, hr, rs, rr,
):
    gx, gy, gz = lax.axis_index("gx"), lax.axis_index("gy"), lax.axis_index("gz")
    yy, xhi = gz // 2, lax.rem(gz, 2)

    own_copies = [
        pltpu.make_async_copy(src, E.at[a, 1, 3:7, 0:8, :], in_sem.at[a])
        for a, src in enumerate((bits_hbm, dis_hbm))
    ]
    for cp in own_copies:
        cp.start()

    def neighbour(d):
        return {
            "gx": lax.rem(gx + d[0] + 8, 8),
            "gy": lax.rem(gy + d[1] + 4, 4),
            "gz": lax.rem(gz + d[2] + 16, 16),
        }

    x8 = xhi * 4 + gy

    def peer(phase, k):
        if phase == 0:
            t = lax.rem(x8 + k, 8)
            return {"gx": gx, "gy": lax.rem(t, 4), "gz": yy * 2 + t // 4}
        if phase == 1:
            return {"gx": lax.rem(gx + k, 8), "gy": gy, "gz": gz}
        return {"gx": gx, "gy": gy, "gz": lax.rem(yy + k, 8) * 2 + xhi}

    ranks = (x8, gx, yy)

    barrier = pltpu.get_barrier_semaphore()
    n_sig = 0
    for d in DIRS:
        pl.semaphore_signal(barrier, inc=1, device_id=neighbour(d), device_id_type=MESH)
        n_sig += 1
    for phase in range(3):
        for k in range(1, 8):
            pl.semaphore_signal(barrier, inc=1, device_id=peer(phase, k), device_id_type=MESH)
            n_sig += 1

    lane = lax.broadcasted_iota(I32, (8, 128), 1)
    row = lax.broadcasted_iota(I32, (8, 128), 0)
    l0, l127 = lane == 0, lane == 127
    r0, r7 = row == 0, row == 7

    for cp in own_copies:
        cp.wait()
    pl.semaphore_wait(barrier, n_sig)

    halo = []
    for i, (dx, dy, dz) in enumerate(DIRS):
        n = 3 - abs(dy) - abs(dz)
        if dx == 1:
            xs, xd = slice(7 - n, 7), slice(3 - n, 3)
        elif dx == -1:
            xs, xd = slice(3, 3 + n), slice(7, 7 + n)
        else:
            xs, xd = slice(3, 7), slice(3, 7)
        if dz == 1:
            ws, wd = slice(7, 8), slice(15, 16)
        elif dz == -1:
            ws, wd = slice(0, 1), slice(8, 9)
        else:
            ws, wd = slice(0, 8), slice(0, 8)
        cp = pltpu.make_async_remote_copy(
            src_ref=E.at[:, 1, xs, ws, :],
            dst_ref=E.at[:, 1 - dy, xd, wd, :],
            send_sem=hs.at[i],
            recv_sem=hr.at[i],
            device_id=neighbour((dx, dy, dz)),
            device_id_type=MESH,
        )
        cp.start()
        halo.append(cp)
    for cp in halo:
        cp.wait_recv()

    def tile(a, t, xi, second):
        return E[a, t, xi + 1, (8 if second else 0) : (16 if second else 8), :]

    def pack_y(a, second):
        out = jnp.zeros((8, 128), I32)
        for xi in range(8):
            left, own, right = (tile(a, t, xi, second) for t in range(3))
            m1 = jnp.where(lane >= 64, left, own)
            m2 = jnp.where(lane >= 64, own, right)
            slot = lane - 16 * xi
            out = jnp.where((slot >= 0) & (slot < 8), roll(m1, 16 * xi - 125, 1), out)
            out = jnp.where((slot >= 8) & (slot < 16), roll(m2, 16 * xi + 8 - 126, 1), out)
        return out

    def up_down(main, second):
        up = roll(jnp.where(r0, second, main), 7, 0)
        down = roll(jnp.where(r7, second, main), 1, 0)
        return up, down

    def z_words(word, up, down):
        zp = (srl(word, 1) & 0x77777777) | (up << 3 & -0x77777778)
        zm = (word << 1 & -0x11111112) | (srl(down, 3) & 0x11111111)
        return zp, zm

    def sides(a, xi, second):
        left, own, right = (tile(a, t, xi, second) for t in range(3))
        return roll(jnp.where(l127, left, own), 1, 1), roll(jnp.where(l0, right, own), 127, 1)

    def energy(word, shift):
        return ((srl(word, shift) & 255).astype(F32) + 0.5) * (1.0 / 64.0) - 2.0

    def zshift(depth, unit):
        return jnp.where(row < 4, unit * (depth - 1), unit * (4 - depth))

    for xi in range(8):
        main, second = tile(0, 1, xi, False), tile(0, 1, xi, True)
        up, down = up_down(main, second)
        zp, zm = z_words(main, up, down)
        ym, yp = sides(0, xi, False)
        planes = count_bits(tile(0, 1, xi + 1, False), tile(0, 1, xi - 1, False), yp, ym, zp, zm)
        for j in range(4):
            NM[xi, j] = nibbles(planes, main, j)
            e = energy(tile(1, 1, xi, False), 8 * j)
            EPM[xi, j] = (6.0 + e) * C1
            EMM[xi, j] = (6.0 - e) * C1
            E2M[xi, j] = e * C2
        if 1 <= xi <= 6:
            up, down = up_down(second, main)
            zp, zm = z_words(second, up, down)
            ym, yp = sides(0, xi, True)
            planes = count_bits(tile(0, 1, xi + 1, True), tile(0, 1, xi - 1, True), yp, ym, zp, zm)
            NZ1[xi - 1] = nibbles(planes, second, zshift(1, 1))
            e = energy(tile(1, 1, xi, True), zshift(1, 8))
            EPZ1[xi - 1] = (6.0 + e) * C1
            EMZ1[xi - 1] = (6.0 - e) * C1
            if 2 <= xi <= 5:
                E2Z[xi - 2] = e * C2
                NZ2[xi - 2] = nibbles(planes, second, zshift(2, 1))
                e = energy(tile(1, 1, xi, True), zshift(2, 8))
                EPZ2[xi - 2] = (6.0 + e) * C1
                EMZ2[xi - 2] = (6.0 - e) * C1

    yw, yw2 = pack_y(0, False), pack_y(0, True)
    yd, yd2 = pack_y(1, False), pack_y(1, True)

    def y_planes(word, up, down):
        zp, zm = z_words(word, up, down)
        return count_bits(roll(word, 1, 1), roll(word, 127, 1), roll(word, 16, 1), roll(word, 112, 1), zp, zm)

    planes = y_planes(yw, *up_down(yw, yw2))
    for j in range(4):
        NY[j] = nibbles(planes, yw, j)
        e = energy(yd, 8 * j)
        EPY[j] = (6.0 + e) * C1
        EMY[j] = (6.0 - e) * C1
        E2Y[j] = e * C2
    planes = y_planes(yw2, *up_down(yw2, yw))
    NY2[...] = nibbles(planes, yw2, zshift(1, 1))
    e = energy(yd2, zshift(1, 8))
    EPY2[...] = (6.0 + e) * C1
    EMY2[...] = (6.0 - e) * C1

    col = lane & 15

    def inner(y):
        return jnp.where(col == 3, roll(y, 121, 1), y)

    def first_order(word, ep, em, sh):
        t = srl(word, sh)
        return jnp.where((t & 8) != 0, ep, em) - C2 * (t & 7).astype(F32)

    def sign(word, sh):
        return jnp.where((srl(word, sh) & 8) != 0, 1.0, -1.0).astype(F32)

    def around(get, edge, ins, xi, j, sub):
        c = get(xi, j)
        a = roll(ins, 127 - (16 * xi + 2), 1)
        s = get(xi + 1, j) + get(xi - 1, j)
        s = s + roll(jnp.where(l127, a, c), 1, 1) + roll(jnp.where(l0, a, c), 127, 1)
        zp = get(xi, j + 1) if j < 3 else roll(jnp.where(r0, edge(xi), get(xi, 0)), 7, 0)
        zm = get(xi, j - 1) if j > 0 else roll(jnp.where(r7, edge(xi), get(xi, 3)), 1, 0)
        return c, s + (zp + zm)

    def second_main(r, xi, j):
        c, s = around(
            lambda x, k: V1M[r, x, k], lambda x: V1Z1[r, x - 1], V1YI[r, j], xi, j, None
        )
        sg = sign(NM[xi, j], 4 * r)
        return c, sg, E2M[xi, j] * c - C2 * s - sg

    def pass_a(r, carry):
        sh = 4 * r
        for xi in range(8):
            for j in range(4):
                V1M[r, xi, j] = first_order(NM[xi, j], EPM[xi, j], EMM[xi, j], sh)
        for xi in range(6):
            V1Z1[r, xi] = first_order(NZ1[xi], EPZ1[xi], EMZ1[xi], sh)
        for xi in range(4):
            V1Z2[r, xi] = first_order(NZ2[xi], EPZ2[xi], EMZ2[xi], sh)
        for j in range(4):
            y = first_order(NY[j], EPY[j], EMY[j], sh)
            V1Y[r, j] = y
            V1YI[r, j] = inner(y)
        y = first_order(NY2[...], EPY2[...], EMY2[...], sh)
        V1Y2[r] = y
        V1Y2I[r] = inner(y)
        a1 = jnp.zeros((8, 128), F32)
        a2 = jnp.zeros((8, 128), F32)
        a3 = jnp.zeros((8, 128), F32)
        for x in range(4):
            for j in range(4):
                v1, sg, v2 = second_main(r, x + 2, j)
                V2M[r, x + 1, j] = v2
                prev[r, x, pl.ds(j, 8, stride=4), :] = v2
                a1 = a1 + sg * v1
                a2 = a2 + v1 * v1
                a3 = a3 + v1 * v2
        a3 = 2.0 * a3 - a1
        a2 = 2.0 * a2 - float(LOCAL // 1024)
        for m, acc in enumerate((a1, a2, a3)):
            ACC[m, pl.ds(r, 1), :] = jnp.sum(acc, axis=0, keepdims=True)
        return carry

    lax.fori_loop(0, 8, pass_a, 0)

    mine = jnp.zeros((8, 128), F32)
    for m in range(3):
        tot = jnp.sum(ACC[m], axis=1, keepdims=True)
        mine = mine + jnp.where(lane == row + 8 * m, jnp.broadcast_to(tot, (8, 128)), 0.0)

    def sum_rows(t):
        t = t + roll(t, 4, 0)
        t = t + roll(t, 2, 0)
        return t + roll(t, 1, 0)

    mine = sum_rows(mine)

    def send(phase, value):
        S[phase] = value
        copies = []
        for k in range(1, 8):
            cp = pltpu.make_async_remote_copy(
                src_ref=S.at[phase, 0:1, :],
                dst_ref=G.at[phase, pl.ds(ranks[phase], 1), :],
                send_sem=rs.at[phase, k],
                recv_sem=rr.at[phase, k],
                device_id=peer(phase, k),
                device_id_type=MESH,
            )
            cp.start()
            copies.append(cp)
        return copies

    def collect(phase, copies, value):
        for cp in copies:
            cp.wait_recv()
        return sum_rows(jnp.where(row == ranks[phase], value, G[phase]))

    sends0 = send(0, mine)

    def pass_b(r, carry):
        for xi, slot in ((1, 0), (6, 5)):
            for j in range(4):
                V2M[r, slot, j] = second_main(r, xi, j)[2]
        for x in range(4):
            xi = x + 2
            c = V1Z1[r, xi - 1]
            a = roll(V1Y2I[r], 127 - (16 * xi + 2), 1)
            s = V1Z1[r, xi] + V1Z1[r, xi - 2]
            s = s + roll(jnp.where(l127, a, c), 1, 1) + roll(jnp.where(l0, a, c), 127, 1)
            ins = jnp.where(r7, roll(V1M[r, xi, 0], 7, 0), roll(V1M[r, xi, 3], 1, 0))
            s = s + (V1Z2[r, x] + ins)
            V2Z[r, x] = E2Z[x] * c - C2 * s - sign(NZ1[xi - 1], 4 * r)
        for j in range(4):
            c = V1Y[r, j]
            s = roll(c, 1, 1) + roll(c, 127, 1) + (roll(c, 16, 1) + roll(c, 112, 1))
            zp = V1Y[r, j + 1] if j < 3 else roll(jnp.where(r0, V1Y2[r], V1Y[r, 0]), 7, 0)
            zm = V1Y[r, j - 1] if j > 0 else roll(jnp.where(r7, V1Y2[r], V1Y[r, 3]), 1, 0)
            s = s + (zp + zm)
            V2YI[r, j] = inner(E2Y[j] * c - C2 * s - sign(NY[j], 4 * r))
        return carry

    lax.fori_loop(0, 8, pass_b, 0)
    total = collect(0, sends0, mine)
    sends1 = send(1, total)

    def pass_c(r, carry):
        for x in range(4):
            for j in range(4):
                c, s = around(
                    lambda xi, k: V2M[r, xi - 1, k], lambda xi: V2Z[r, xi - 2], V2YI[r, j], x + 2, j, None
                )
                cur[r, x, pl.ds(j, 8, stride=4), :] = E2M[x + 2, j] * c - C2 * s - V1M[r, x + 2, j]
        return carry

    lax.fori_loop(0, 8, pass_c, 0)
    total1 = collect(1, sends1, total)
    sends2 = send(2, total1)
    total2 = collect(2, sends2, total1) * (1.0 / NSITES)
    out = jnp.where(r0, total2, jnp.where(row == 1, roll(total2, 120, 1), roll(total2, 112, 1)))
    mom[...] = out[:3, :8]
    for cp in halo + sends0 + sends1 + sends2:
        cp.wait_send()


def vm(*shape, dtype=F32):
    return pltpu.VMEM(shape + (8, 128), dtype)


def per_device(probe_bits, disorder_levels):
    dma = pltpu.SemaphoreType.DMA
    return pl.pallas_call(
        kernel,
        out_shape=(
            jax.ShapeDtypeStruct((3, 8), F32),
            jax.ShapeDtypeStruct((8, 4, 32, 128), F32),
            jax.ShapeDtypeStruct((8, 4, 32, 128), F32),
        ),
        in_specs=[pl.BlockSpec(memory_space=pltpu.HBM)] * 2,
        out_specs=(pl.BlockSpec(memory_space=pltpu.VMEM),) * 3,
        scratch_shapes=[
            pltpu.VMEM((2, 3, 10, 16, 128), I32),
            vm(8, 4, dtype=I32), vm(6, dtype=I32), vm(4, dtype=I32), vm(4, dtype=I32), vm(dtype=I32),
            vm(8, 4), vm(8, 4), vm(8, 4),
            vm(6), vm(6), vm(4), vm(4), vm(4),
            vm(4), vm(4), vm(4), vm(), vm(),
            vm(8, 8, 4), vm(8, 6), vm(8, 4), vm(8, 4), vm(8, 4), vm(8), vm(8),
            vm(8, 6, 4), vm(8, 4), vm(8, 4),
            vm(3), vm(3), vm(3),
            dma((2,)), dma((26,)), dma((26,)), dma((3, 8)), dma((3, 8)),
        ],
        compiler_params=pltpu.CompilerParams(
            collective_id=0, has_side_effects=True, vmem_limit_bytes=24 * 1024 * 1024
        ),
    )(pltpu.with_memory_space_constraint(probe_bits, pltpu.HBM), pltpu.with_memory_space_constraint(disorder_levels, pltpu.HBM))


def solution(mesh):
    return jax.shard_map(
        per_device,
        mesh=mesh,
        in_specs=(P("gx", "gz", "gy"), P("gx", "gz", "gy")),
        out_specs=(P(), P(None, "gx", "gz", "gy"), P(None, "gx", "gz", "gy")),
        check_vma=False,
    )
```

time: 103 us -> 37.9 us (0.37)
  the two profiles are of different devices: /device:TPU:6 before, /device:TPU:1 now
where the time goes in v1:
time: 37.9 us; the launch traced here: 37.5 us
  Pallas kernels  34.6 us (91%)
  local copies, waits for them, and re-layouts  2.17 us (6%)
  between operations  0.64 us (2%)
    pallas_call x1, Pallas kernels, per_device(): pl.pallas_call(kernel, out_shape=(jax.ShapeDtypeStruct((3, 8), F32), jax....  34.6 us
    unnamed x3, local copies, waits for them, and re-layouts  2.17 us

profile of v1, /device:TPU:1, one launch (start us, length us, event | category | flops | bytes accessed | tf_op | source)
XLA Modules:
  0.0 37.5 jit_solution(306038655831882995)
XLA Ops:
  0.6 34.6 %shard_map.49 = (f32[3,8]{1,0:T(4,128)S(1)}, f32[8,4,32,128]{3,2,1,0:T(8,128)S(1)}, f32[8,4,32,128]{3,2,1,0:T(8,128)S(1)}) custom-call(s32[4,8,128]{2,1,0:T(8,128)} %bits_hbm.1, s32[4,8,128]{2,1,0:T(8,128)} %dis_hbm.1), custom_call_target="tpu_custom_call" | custom-call | tf_op jit(solution)/shard_map/pallas_call | solution.py:374
  35.3 0.6 %copy.8 = f32[3,8]{1,0:T(4,128)} copy(f32[3,8]{1,0:T(4,128)S(1)} %get-tuple-element.6) | data formatting | bytes 192
  35.9 0.8 %copy.9 = f32[8,4,32,128]{3,2,1,0:T(8,128)} copy(f32[8,4,32,128]{3,2,1,0:T(8,128)S(1)} %get-tuple-element.7) | data formatting | bytes 1048576
  36.7 0.8 %copy.10 = f32[8,4,32,128]{3,2,1,0:T(8,128)} copy(f32[8,4,32,128]{3,2,1,0:T(8,128)S(1)} %get-tuple-element.8) | data formatting | bytes 1048576

commit v2 on v1

--- a/solution.py
+++ b/solution.py
@@ -61,8 +61,8 @@
     bits_hbm, dis_hbm, mom, prev, cur,
     E, NM, NZ1, NZ2, NY, NY2,
     EPM, EMM, E2M, EPZ1, EMZ1, EPZ2, EMZ2, E2Z, EPY, EMY, E2Y, EPY2, EMY2,
-    V1M, V1Z1, V1Z2, V1Y, V1YI, V1Y2I, V1Y2, V2M, V2Z, V2YI, ACC, S, G,
-    in_sem, hs, hr, rs, rr,
+    V1M, V1Z1, V1Z2, V1Y, V1YI, V1Y2I, V1Y2, V2M, V2Z, V2YI, ACC, S, GP, GL,
+    in_sem, hs, hr, ps, pr, ls, lr,
 ):
     gx, gy, gz = lax.axis_index("gx"), lax.axis_index("gy"), lax.axis_index("gz")
     yy, xhi = gz // 2, lax.rem(gz, 2)
@@ -81,27 +81,38 @@
             "gz": lax.rem(gz + d[2] + 16, 16),
         }
 
-    x8 = xhi * 4 + gy
-
-    def peer(phase, k):
-        if phase == 0:
-            t = lax.rem(x8 + k, 8)
-            return {"gx": gx, "gy": lax.rem(t, 4), "gz": yy * 2 + t // 4}
-        if phase == 1:
-            return {"gx": lax.rem(gx + k, 8), "gy": gy, "gz": gz}
-        return {"gx": gx, "gy": gy, "gz": lax.rem(yy + k, 8) * 2 + xhi}
-
-    ranks = (x8, gx, yy)
+    core = lax.rem(gy, 2)
+    px = xhi * 2 + gy // 2
+    place = yy * 4 + px
+
+    def plane_peer(k, c):
+        t = lax.rem(place + k, 32)
+        q = lax.rem(t, 4)
+        return {"gx": gx, "gy": lax.rem(q, 2) * 2 + c, "gz": (t // 4) * 2 + q // 2}
+
+    def line_peer(k, c):
+        return {"gx": lax.rem(gx + k, 8), "gy": (gy // 2) * 2 + c, "gz": gz}
 
     barrier = pltpu.get_barrier_semaphore()
-    n_sig = 0
+
+    def greet(device):
+        pl.semaphore_signal(barrier, inc=1, device_id=device, device_id_type=MESH)
+
     for d in DIRS:
-        pl.semaphore_signal(barrier, inc=1, device_id=neighbour(d), device_id_type=MESH)
-        n_sig += 1
-    for phase in range(3):
-        for k in range(1, 8):
-            pl.semaphore_signal(barrier, inc=1, device_id=peer(phase, k), device_id_type=MESH)
-            n_sig += 1
+        greet(neighbour(d))
+    for k in range(1, 8):
+        greet(line_peer(k, 1))
+
+    @pl.when(core == 0)
+    def _():
+        greet(line_peer(0, 1))
+
+    @pl.when(core == 1)
+    def _():
+        for k in range(1, 32):
+            greet(plane_peer(k, 1))
+        for k in range(32):
+            greet(plane_peer(k, 0))
 
     lane = lax.broadcasted_iota(I32, (8, 128), 1)
     row = lax.broadcasted_iota(I32, (8, 128), 0)
@@ -110,7 +121,15 @@
 
     for cp in own_copies:
         cp.wait()
-    pl.semaphore_wait(barrier, n_sig)
+
+    @pl.when(core == 0)
+    def _():
+        pl.semaphore_wait(barrier, 26 + 32)
+
+    @pl.when(core == 1)
+    def _():
+        pl.semaphore_wait(barrier, 26 + 31 + 15)
+
 
     halo = []
     for i, (dx, dy, dz) in enumerate(DIRS):
@@ -297,28 +316,46 @@
 
     mine = sum_rows(mine)
 
-    def send(phase, value):
-        S[phase] = value
-        copies = []
-        for k in range(1, 8):
-            cp = pltpu.make_async_remote_copy(
-                src_ref=S.at[phase, 0:1, :],
-                dst_ref=G.at[phase, pl.ds(ranks[phase], 1), :],
-                send_sem=rs.at[phase, k],
-                recv_sem=rr.at[phase, k],
-                device_id=peer(phase, k),
-                device_id_type=MESH,
-            )
-            cp.start()
-            copies.append(cp)
-        return copies
-
-    def collect(phase, copies, value):
-        for cp in copies:
-            cp.wait_recv()
-        return sum_rows(jnp.where(row == ranks[phase], value, G[phase]))
-
-    sends0 = send(0, mine)
+    slot = place * 2 + core
+
+    def plane_copy(k):
+        return pltpu.make_async_remote_copy(
+            src_ref=S.at[0, 0:1, :],
+            dst_ref=GP.at[pl.ds(slot, 1), :],
+            send_sem=ps.at[k],
+            recv_sem=pr.at[(1 - core) * 32 + k],
+            device_id=plane_peer(k, 1),
+            device_id_type=MESH,
+        )
+
+    def line_copy(k, c):
+        return pltpu.make_async_remote_copy(
+            src_ref=S.at[1, 0:1, :],
+            dst_ref=GL.at[pl.ds(gx, 1), :],
+            send_sem=ls.at[c * 8 + k],
+            recv_sem=lr.at[c * 8 + k],
+            device_id=line_peer(k, c),
+            device_id_type=MESH,
+        )
+
+    def plane_arrived(q):
+        return pltpu.make_async_remote_copy(
+            src_ref=S.at[0, 0:1, :],
+            dst_ref=GP.at[0:1, :],
+            send_sem=ps.at[0],
+            recv_sem=pr.at[q],
+            device_id=plane_peer(1, 1),
+            device_id_type=MESH,
+        ).wait_recv()
+
+    S[0] = mine
+    for k in range(1, 32):
+        plane_copy(k).start()
+
+    @pl.when(core == 0)
+    def _():
+        plane_copy(0).start()
+
 
     def pass_b(r, carry):
         for xi, slot in ((1, 0), (6, 5)):
@@ -343,8 +380,6 @@
         return carry
 
     lax.fori_loop(0, 8, pass_b, 0)
-    total = collect(0, sends0, mine)
-    sends1 = send(1, total)
 
     def pass_c(r, carry):
         for x in range(4):
@@ -356,13 +391,57 @@
         return carry
 
     lax.fori_loop(0, 8, pass_c, 0)
-    total1 = collect(1, sends1, total)
-    sends2 = send(2, total1)
-    total2 = collect(2, sends2, total1) * (1.0 / NSITES)
-    out = jnp.where(r0, total2, jnp.where(row == 1, roll(total2, 120, 1), roll(total2, 112, 1)))
+
+    @pl.when(core == 1)
+    def _():
+        for q in range(1, 64):
+            plane_arrived(q)
+        acc = jnp.zeros((8, 128), F32)
+        for q in range(8):
+            acc = acc + jnp.where(row + 8 * q == slot, mine, GP[8 * q : 8 * q + 8, :])
+        S[1] = sum_rows(acc)
+        for k in range(8):
+            line_copy(k, 0).start()
+        for k in range(1, 8):
+            line_copy(k, 1).start()
+        for k in range(1, 8):
+            line_copy(k, 1).wait_recv()
+        GL[pl.ds(gx, 1), :] = S[1, 0:1, :]
+
+    @pl.when(core == 0)
+    def _():
+        for k in range(8):
+            line_copy(k, 0).wait_recv()
+
+    total = sum_rows(GL[...]) * (1.0 / NSITES)
+    out = jnp.where(r0, total, jnp.where(row == 1, roll(total, 120, 1), roll(total, 112, 1)))
     mom[...] = out[:3, :8]
-    for cp in halo + sends0 + sends1 + sends2:
+    for cp in halo:
         cp.wait_send()
+    for k in range(1, 32):
+        plane_copy(k).wait_send()
+
+    @pl.when(core == 0)
+    def _():
+        plane_copy(0).wait_send()
+
+    @pl.when(core == 1)
+    def _():
+        for k in range(8):
+            line_copy(k, 0).wait_send()
+        for k in range(1, 8):
+            line_copy(k, 1).wait_send()
+
+
+def write_out(mom, prev, cur, mom_out, prev_out, cur_out, sems):
+    copies = [
+        pltpu.make_async_copy(src, dst, sems.at[i])
+        for i, (src, dst) in enumerate(((prev, prev_out), (cur, cur_out), (mom, mom_out)))
+    ]
+    for cp in copies:
+        cp.start()
+    for cp in copies:
+        cp.wait()
 
 
 def vm(*shape, dtype=F32):
@@ -371,13 +450,14 @@
 
 def per_device(probe_bits, disorder_levels):
     dma = pltpu.SemaphoreType.DMA
-    return pl.pallas_call(
+    shapes = (
+        jax.ShapeDtypeStruct((3, 8), F32),
+        jax.ShapeDtypeStruct((8, 4, 32, 128), F32),
+        jax.ShapeDtypeStruct((8, 4, 32, 128), F32),
+    )
+    held = pl.pallas_call(
         kernel,
-        out_shape=(
-            jax.ShapeDtypeStruct((3, 8), F32),
-            jax.ShapeDtypeStruct((8, 4, 32, 128), F32),
-            jax.ShapeDtypeStruct((8, 4, 32, 128), F32),
-        ),
+        out_shape=shapes,
         in_specs=[pl.BlockSpec(memory_space=pltpu.HBM)] * 2,
         out_specs=(pl.BlockSpec(memory_space=pltpu.VMEM),) * 3,
         scratch_shapes=[
@@ -388,13 +468,21 @@
             vm(4), vm(4), vm(4), vm(), vm(),
             vm(8, 8, 4), vm(8, 6), vm(8, 4), vm(8, 4), vm(8, 4), vm(8), vm(8),
             vm(8, 6, 4), vm(8, 4), vm(8, 4),
-            vm(3), vm(3), vm(3),
-            dma((2,)), dma((26,)), dma((26,)), dma((3, 8)), dma((3, 8)),
+            vm(3), vm(2), pltpu.VMEM((64, 128), F32), vm(),
+            dma((2,)), dma((26,)), dma((26,)), dma((32,)), dma((64,)), dma((16,)), dma((16,)),
         ],
         compiler_params=pltpu.CompilerParams(
             collective_id=0, has_side_effects=True, vmem_limit_bytes=24 * 1024 * 1024
         ),
     )(pltpu.with_memory_space_constraint(probe_bits, pltpu.HBM), pltpu.with_memory_space_constraint(disorder_levels, pltpu.HBM))
+    return pl.pallas_call(
+        write_out,
+        out_shape=shapes,
+        in_specs=[pl.BlockSpec(memory_space=pltpu.VMEM)] * 3,
+        out_specs=(pl.BlockSpec(memory_space=pltpu.HBM),) * 3,
+        scratch_shapes=[dma((3,))],
+        compiler_params=pltpu.CompilerParams(vmem_limit_bytes=4 * 1024 * 1024),
+    )(*held)
 
 
 def solution(mesh):

time: 37.9 us -> 36.1 us (0.953)
  local copies, waits for them, and re-layouts: 2.17 us -> 0 us
  Pallas kernels: 34.6 us -> 35.2 us
    unnamed x3 -> x0, local copies, waits for them, and re-layouts: 2.17 us -> none
    pallas_call x1 -> x2, Pallas kernels: 34.6 us -> 35.2 us  [the longest x1 34.2 us: per_device(): pl.pallas_call(kernel, out_shape=shapes, in_specs=[pl.BlockSpec(memory_sp...]
where the time goes in v2:
time: 36.1 us; the launch traced here: 35.9 us
  Pallas kernels  35.2 us (98%)
  between operations  0.64 us (2%)
    pallas_call x1, Pallas kernels, per_device(): pl.pallas_call(kernel, out_shape=shapes, in_specs=[pl.BlockSpec(memory_sp...  34.2 us
    pallas_call x1, Pallas kernels, per_device(): pl.pallas_call(write_out, out_shape=shapes, in_specs=[pl.BlockSpec(memory...  1 us

profile of v2, /device:TPU:1, one launch (start us, length us, event | category | flops | bytes accessed | tf_op | source)
XLA Modules:
  0.0 35.9 jit_solution(9993783571864752631)
XLA Ops:
  0.6 34.2 %shard_map.49 = (f32[3,8]{1,0:T(4,128)S(1)}, f32[8,4,32,128]{3,2,1,0:T(8,128)S(1)}, f32[8,4,32,128]{3,2,1,0:T(8,128)S(1)}) custom-call(s32[4,8,128]{2,1,0:T(8,128)} %bits_hbm.1, s32[4,8,128]{2,1,0:T(8,128)} %dis_hbm.1), custom_call_target="tpu_custom_call" | custom-call | tf_op jit(solution)/shard_map/pallas_call | solution.py:458
  34.9 1.0 %shard_map.50 = (f32[3,8]{1,0:T(4,128)}, f32[8,4,32,128]{3,2,1,0:T(8,128)}, f32[8,4,32,128]{3,2,1,0:T(8,128)}) custom-call(f32[3,8]{1,0:T(4,128)S(1)} %get-tuple-element.6.mom, f32[8,4,32,128]{3,2,1,0:T(8,128)S(1)} %get-tuple-element.7.prev, f32[8,4,32,128]{3,2,1,0:T(8,128)S(1)} %get-tuple-element.8.cur), custom_call_target="tpu_custom_call" | custom-call | tf_op jit(solution)/shard_map/pallas_call | solution.py:478

commit v3 on v2

--- a/solution.py
+++ b/solution.py
@@ -8,9 +8,7 @@
 F32 = jnp.float32
 I32 = jnp.int32
 MESH = pl.DeviceIdType.MESH
-C1 = 1.0 / 8.4
 C2 = 2.0 / 8.4
-SIZES = {"gx": 8, "gy": 4, "gz": 16}
 NSITES = 32 * 512 * 512
 LOCAL = 4 * 32 * 128
 
@@ -34,13 +32,7 @@
     return pltpu.roll(a, n % a.shape[axis], axis)
 
 
-def count_bits(a, b, c, d, e, f):
-    x = a ^ b
-    s1 = x ^ c
-    c1 = (a & b) | (c & x)
-    y = d ^ e
-    s2 = y ^ f
-    c2 = (d & e) | (f & y)
+def add_counts(s1, c1, s2, c2):
     h = s1 & s2
     z = c1 ^ c2
     return s1 ^ s2, z ^ h, (c1 & c2) | (h & z)
@@ -59,7 +51,7 @@
 
 def kernel(
     bits_hbm, dis_hbm, mom, prev, cur,
-    E, NM, NZ1, NZ2, NY, NY2,
+    E, LAT, SG, NM, NZ1, NZ2, NY, NY2,
     EPM, EMM, E2M, EPZ1, EMZ1, EPZ2, EMZ2, E2Z, EPY, EMY, E2Y, EPY2, EMY2,
     V1M, V1Z1, V1Z2, V1Y, V1YI, V1Y2I, V1Y2, V2M, V2Z, V2YI, ACC, S, GP, GL,
     in_sem, hs, hr, ps, pr, ls, lr,
@@ -74,24 +66,28 @@
     for cp in own_copies:
         cp.start()
 
+    near_x = {d: lax.rem(gx + d + 8, 8) if d else gx for d in (-1, 0, 1)}
+    near_y = {d: lax.rem(gy + d + 4, 4) if d else gy for d in (-1, 0, 1)}
+    near_z = {d: lax.rem(gz + d + 16, 16) if d else gz for d in (-1, 0, 1)}
+
     def neighbour(d):
-        return {
-            "gx": lax.rem(gx + d[0] + 8, 8),
-            "gy": lax.rem(gy + d[1] + 4, 4),
-            "gz": lax.rem(gz + d[2] + 16, 16),
-        }
+        return {"gx": near_x[d[0]], "gy": near_y[d[1]], "gz": near_z[d[2]]}
 
     core = lax.rem(gy, 2)
+    pair = gy - core
     px = xhi * 2 + gy // 2
     place = yy * 4 + px
+    line = [gx] + [lax.rem(gx + k, 8) for k in range(1, 8)]
+    row_y = [yy * 2] + [lax.rem(yy + k, 8) * 2 for k in range(1, 8)]
+    row_x = [px] + [lax.rem(px + k, 4) for k in range(1, 4)]
+    row_h = [q // 2 for q in row_x]
+    row_p = [(q - 2 * h) * 2 for q, h in zip(row_x, row_h)]
 
     def plane_peer(k, c):
-        t = lax.rem(place + k, 32)
-        q = lax.rem(t, 4)
-        return {"gx": gx, "gy": lax.rem(q, 2) * 2 + c, "gz": (t // 4) * 2 + q // 2}
+        return {"gx": gx, "gy": row_p[k % 4] + c, "gz": row_y[k // 4] + row_h[k % 4]}
 
     def line_peer(k, c):
-        return {"gx": lax.rem(gx + k, 8), "gy": (gy // 2) * 2 + c, "gz": gz}
+        return {"gx": line[k], "gy": pair + c, "gz": gz}
 
     barrier = pltpu.get_barrier_semaphore()
 
@@ -156,8 +152,9 @@
         )
         cp.start()
         halo.append(cp)
-    for cp in halo:
-        cp.wait_recv()
+    for cp, d in zip(halo, DIRS):
+        if d[2] == 0:
+            cp.wait_recv()
 
     def tile(a, t, xi, second):
         return E[a, t, xi + 1, (8 if second else 0) : (16 if second else 8), :]
@@ -188,92 +185,115 @@
         return roll(jnp.where(l127, left, own), 1, 1), roll(jnp.where(l0, right, own), 127, 1)
 
     def energy(word, shift):
-        return ((srl(word, shift) & 255).astype(F32) + 0.5) * (1.0 / 64.0) - 2.0
+        return (srl(word, shift) & 255).astype(F32)
 
     def zshift(depth, unit):
         return jnp.where(row < 4, unit * (depth - 1), unit * (4 - depth))
+
+    def weights(word, shift):
+        lev = energy(word, shift)
+        half = lev * (1.0 / 128.0)
+        return half + (3.0 - 255.0 / 256.0 - 8.0), (3.0 + 255.0 / 256.0) - half
+
+    def slope(word, shift):
+        return energy(word, shift) * (C2 / 64.0) - (C2 * 255.0 / 128.0)
+
+    def half_count(a, b, c):
+        x = a ^ b
+        return x ^ c, (a & b) | (c & x)
+
+    for xi in range(8):
+        dis = tile(1, 1, xi, False)
+        for j in range(4):
+            EPM[xi, j], EMM[xi, j] = weights(dis, 8 * j)
+            if 1 <= xi <= 6:
+                E2M[xi, j] = slope(dis, 8 * j)
+        ym, yp = sides(0, xi, False)
+        LAT[xi, 0], LAT[xi, 1] = half_count(tile(0, 1, xi + 1, False), tile(0, 1, xi - 1, False), yp)
+        LAT[xi, 2] = ym
+    yw, yd = pack_y(0, False), pack_y(1, False)
+    for j in range(4):
+        EPY[j], EMY[j] = weights(yd, 8 * j)
+        E2Y[j] = slope(yd, 8 * j)
+    for cp, d in zip(halo, DIRS):
+        if d[2] != 0:
+            cp.wait_recv()
 
     for xi in range(8):
         main, second = tile(0, 1, xi, False), tile(0, 1, xi, True)
         up, down = up_down(main, second)
         zp, zm = z_words(main, up, down)
-        ym, yp = sides(0, xi, False)
-        planes = count_bits(tile(0, 1, xi + 1, False), tile(0, 1, xi - 1, False), yp, ym, zp, zm)
+        planes = add_counts(LAT[xi, 0], LAT[xi, 1], *half_count(LAT[xi, 2], zp, zm))
         for j in range(4):
             NM[xi, j] = nibbles(planes, main, j)
-            e = energy(tile(1, 1, xi, False), 8 * j)
-            EPM[xi, j] = (6.0 + e) * C1
-            EMM[xi, j] = (6.0 - e) * C1
-            E2M[xi, j] = e * C2
         if 1 <= xi <= 6:
             up, down = up_down(second, main)
             zp, zm = z_words(second, up, down)
             ym, yp = sides(0, xi, True)
-            planes = count_bits(tile(0, 1, xi + 1, True), tile(0, 1, xi - 1, True), yp, ym, zp, zm)
+            dis = tile(1, 1, xi, True)
+            planes = add_counts(
+                *half_count(tile(0, 1, xi + 1, True), tile(0, 1, xi - 1, True), yp),
+                *half_count(ym, zp, zm),
+            )
             NZ1[xi - 1] = nibbles(planes, second, zshift(1, 1))
-            e = energy(tile(1, 1, xi, True), zshift(1, 8))
-            EPZ1[xi - 1] = (6.0 + e) * C1
-            EMZ1[xi - 1] = (6.0 - e) * C1
+            EPZ1[xi - 1], EMZ1[xi - 1] = weights(dis, zshift(1, 8))
             if 2 <= xi <= 5:
-                E2Z[xi - 2] = e * C2
+                E2Z[xi - 2] = slope(dis, zshift(1, 8))
                 NZ2[xi - 2] = nibbles(planes, second, zshift(2, 1))
-                e = energy(tile(1, 1, xi, True), zshift(2, 8))
-                EPZ2[xi - 2] = (6.0 + e) * C1
-                EMZ2[xi - 2] = (6.0 - e) * C1
-
-    yw, yw2 = pack_y(0, False), pack_y(0, True)
-    yd, yd2 = pack_y(1, False), pack_y(1, True)
+                EPZ2[xi - 2], EMZ2[xi - 2] = weights(dis, zshift(2, 8))
+
+    yw2, yd2 = pack_y(0, True), pack_y(1, True)
 
     def y_planes(word, up, down):
         zp, zm = z_words(word, up, down)
-        return count_bits(roll(word, 1, 1), roll(word, 127, 1), roll(word, 16, 1), roll(word, 112, 1), zp, zm)
+        return add_counts(
+            *half_count(roll(word, 1, 1), roll(word, 127, 1), roll(word, 16, 1)),
+            *half_count(roll(word, 112, 1), zp, zm),
+        )
 
     planes = y_planes(yw, *up_down(yw, yw2))
     for j in range(4):
         NY[j] = nibbles(planes, yw, j)
-        e = energy(yd, 8 * j)
-        EPY[j] = (6.0 + e) * C1
-        EMY[j] = (6.0 - e) * C1
-        E2Y[j] = e * C2
     planes = y_planes(yw2, *up_down(yw2, yw))
     NY2[...] = nibbles(planes, yw2, zshift(1, 1))
-    e = energy(yd2, zshift(1, 8))
-    EPY2[...] = (6.0 + e) * C1
-    EMY2[...] = (6.0 - e) * C1
+    EPY2[...], EMY2[...] = weights(yd2, zshift(1, 8))
 
     col = lane & 15
 
     def inner(y):
-        return jnp.where(col == 3, roll(y, 121, 1), y)
+        return jnp.where(col == 1, roll(y, 119, 1), y)
+
+    def top(word, sh):
+        return word << jnp.full(word.shape, sh, I32)
 
     def first_order(word, ep, em, sh):
-        t = srl(word, sh)
-        return jnp.where((t & 8) != 0, ep, em) - C2 * (t & 7).astype(F32)
+        t = top(word, sh)
+        q = lax.shift_right_arithmetic(t, jnp.full(t.shape, 28, I32)).astype(F32)
+        return jnp.where(t < 0, ep, em) - q
 
     def sign(word, sh):
-        return jnp.where((srl(word, sh) & 8) != 0, 1.0, -1.0).astype(F32)
-
-    def around(get, edge, ins, xi, j, sub):
+        return jnp.where(top(word, sh) < 0, 1.0, -1.0).astype(F32)
+
+    def around(get, edge, ins, xi, j):
         c = get(xi, j)
-        a = roll(ins, 127 - (16 * xi + 2), 1)
+        a = roll(ins, 0 - (16 * xi + 2), 1)
         s = get(xi + 1, j) + get(xi - 1, j)
-        s = s + roll(jnp.where(l127, a, c), 1, 1) + roll(jnp.where(l0, a, c), 127, 1)
+        s = s + (jnp.where(l0, a, roll(c, 1, 1)) + jnp.where(l127, a, roll(c, 127, 1)))
         zp = get(xi, j + 1) if j < 3 else roll(jnp.where(r0, edge(xi), get(xi, 0)), 7, 0)
         zm = get(xi, j - 1) if j > 0 else roll(jnp.where(r7, edge(xi), get(xi, 3)), 1, 0)
         return c, s + (zp + zm)
 
-    def second_main(r, xi, j):
-        c, s = around(
-            lambda x, k: V1M[r, x, k], lambda x: V1Z1[r, x - 1], V1YI[r, j], xi, j, None
-        )
-        sg = sign(NM[xi, j], 4 * r)
-        return c, sg, E2M[xi, j] * c - C2 * s - sg
-
-    def pass_a(r, carry):
-        sh = 4 * r
+    def second_main(r, xi, j, sg):
+        c, s = around(lambda x, k: V1M[r, x, k], lambda x: V1Z1[r, x - 1], V1YI[r, j], xi, j)
+        return c, (E2M[xi, j] * c - C2 * s) * C2 - sg
+
+    def pass_a1(r):
+        sh = 28 - 4 * r
         for xi in range(8):
             for j in range(4):
                 V1M[r, xi, j] = first_order(NM[xi, j], EPM[xi, j], EMM[xi, j], sh)
+                if 2 <= xi <= 5:
+                    SG[r, xi - 2, j] = sign(NM[xi, j], sh)
         for xi in range(6):
             V1Z1[r, xi] = first_order(NZ1[xi], EPZ1[xi], EMZ1[xi], sh)
         for xi in range(4):
@@ -285,24 +305,35 @@
         y = first_order(NY2[...], EPY2[...], EMY2[...], sh)
         V1Y2[r] = y
         V1Y2I[r] = inner(y)
+
+    def pass_a2(r):
         a1 = jnp.zeros((8, 128), F32)
         a2 = jnp.zeros((8, 128), F32)
         a3 = jnp.zeros((8, 128), F32)
         for x in range(4):
             for j in range(4):
-                v1, sg, v2 = second_main(r, x + 2, j)
+                sg = SG[r, x, j]
+                v1, v2 = second_main(r, x + 2, j, sg)
                 V2M[r, x + 1, j] = v2
                 prev[r, x, pl.ds(j, 8, stride=4), :] = v2
                 a1 = a1 + sg * v1
                 a2 = a2 + v1 * v1
                 a3 = a3 + v1 * v2
-        a3 = 2.0 * a3 - a1
-        a2 = 2.0 * a2 - float(LOCAL // 1024)
-        for m, acc in enumerate((a1, a2, a3)):
+        a3 = (2.0 * C2) * a3 - C2 * a1
+        a2 = (2.0 * C2 * C2) * a2 - float(LOCAL // 1024)
+        for m, acc in enumerate((C2 * a1, a2, a3)):
             ACC[m, pl.ds(r, 1), :] = jnp.sum(acc, axis=0, keepdims=True)
-        return carry
-
-    lax.fori_loop(0, 8, pass_a, 0)
+
+    def probes(one, group):
+        def body(g, carry):
+            for i in range(group):
+                one(g * group + i)
+            return carry
+
+        lax.fori_loop(0, 8 // group, body, 0)
+
+    probes(pass_a1, 4)
+    probes(pass_a2, 4)
 
     mine = jnp.zeros((8, 128), F32)
     for m in range(3):
@@ -357,40 +388,39 @@
         plane_copy(0).start()
 
 
-    def pass_b(r, carry):
-        for xi, slot in ((1, 0), (6, 5)):
+    def pass_b(r):
+        sh = 28 - 4 * r
+        for xi, slot2 in ((1, 0), (6, 5)):
             for j in range(4):
-                V2M[r, slot, j] = second_main(r, xi, j)[2]
+                V2M[r, slot2, j] = second_main(r, xi, j, sign(NM[xi, j], sh))[1]
         for x in range(4):
             xi = x + 2
             c = V1Z1[r, xi - 1]
-            a = roll(V1Y2I[r], 127 - (16 * xi + 2), 1)
+            a = roll(V1Y2I[r], 0 - (16 * xi + 2), 1)
             s = V1Z1[r, xi] + V1Z1[r, xi - 2]
-            s = s + roll(jnp.where(l127, a, c), 1, 1) + roll(jnp.where(l0, a, c), 127, 1)
+            s = s + (jnp.where(l0, a, roll(c, 1, 1)) + jnp.where(l127, a, roll(c, 127, 1)))
             ins = jnp.where(r7, roll(V1M[r, xi, 0], 7, 0), roll(V1M[r, xi, 3], 1, 0))
             s = s + (V1Z2[r, x] + ins)
-            V2Z[r, x] = E2Z[x] * c - C2 * s - sign(NZ1[xi - 1], 4 * r)
+            V2Z[r, x] = (E2Z[x] * c - C2 * s) * C2 - sign(NZ1[xi - 1], sh)
         for j in range(4):
             c = V1Y[r, j]
             s = roll(c, 1, 1) + roll(c, 127, 1) + (roll(c, 16, 1) + roll(c, 112, 1))
             zp = V1Y[r, j + 1] if j < 3 else roll(jnp.where(r0, V1Y2[r], V1Y[r, 0]), 7, 0)
             zm = V1Y[r, j - 1] if j > 0 else roll(jnp.where(r7, V1Y2[r], V1Y[r, 3]), 1, 0)
             s = s + (zp + zm)
-            V2YI[r, j] = inner(E2Y[j] * c - C2 * s - sign(NY[j], 4 * r))
-        return carry
-
-    lax.fori_loop(0, 8, pass_b, 0)
-
-    def pass_c(r, carry):
+            V2YI[r, j] = inner((E2Y[j] * c - C2 * s) * C2 - sign(NY[j], sh))
+
+    def pass_c(r):
         for x in range(4):
             for j in range(4):
                 c, s = around(
-                    lambda xi, k: V2M[r, xi - 1, k], lambda xi: V2Z[r, xi - 2], V2YI[r, j], x + 2, j, None
+                    lambda xi, k: V2M[r, xi - 1, k], lambda xi: V2Z[r, xi - 2], V2YI[r, j], x + 2, j
                 )
-                cur[r, x, pl.ds(j, 8, stride=4), :] = E2M[x + 2, j] * c - C2 * s - V1M[r, x + 2, j]
-        return carry
-
-    lax.fori_loop(0, 8, pass_c, 0)
+                v3 = E2M[x + 2, j] * c - C2 * s - C2 * V1M[r, x + 2, j]
+                cur[r, x, pl.ds(j, 8, stride=4), :] = v3
+
+    probes(pass_b, 2)
+    probes(pass_c, 4)
 
     @pl.when(core == 1)
     def _():
@@ -462,7 +492,7 @@
         out_specs=(pl.BlockSpec(memory_space=pltpu.VMEM),) * 3,
         scratch_shapes=[
             pltpu.VMEM((2, 3, 10, 16, 128), I32),
-            vm(8, 4, dtype=I32), vm(6, dtype=I32), vm(4, dtype=I32), vm(4, dtype=I32), vm(dtype=I32),
+            vm(8, 3, dtype=I32), vm(8, 4, 4), vm(8, 4, dtype=I32), vm(6, dtype=I32), vm(4, dtype=I32), vm(4, dtype=I32), vm(dtype=I32),
             vm(8, 4), vm(8, 4), vm(8, 4),
             vm(6), vm(6), vm(4), vm(4), vm(4),
             vm(4), vm(4), vm(4), vm(), vm(),

time: 36.1 us -> 35 us (0.970)
  Pallas kernels: 35.2 us -> 34.1 us
    pallas_call x1, Pallas kernels: 34.2 us -> 33.1 us  [per_device(): pl.pallas_call(kernel, out_shape=shapes, in_specs=[pl.BlockSpec(memory_sp...]
where the time goes in v3:
time: 35 us; the launch traced here: 34.8 us
  Pallas kernels  34.1 us (97%)
  between operations  0.64 us (2%)
    pallas_call x1, Pallas kernels, per_device(): pl.pallas_call(kernel, out_shape=shapes, in_specs=[pl.BlockSpec(memory_sp...  33.1 us
    pallas_call x1, Pallas kernels, per_device(): pl.pallas_call(write_out, out_shape=shapes, in_specs=[pl.BlockSpec(memory...  1 us

profile of v3, /device:TPU:1, one launch (start us, length us, event | category | flops | bytes accessed | tf_op | source)
XLA Modules:
  0.0 34.8 jit_solution(56381588404063119)
XLA Ops:
  0.6 33.1 %shard_map.49 = (f32[3,8]{1,0:T(4,128)S(1)}, f32[8,4,32,128]{3,2,1,0:T(8,128)S(1)}, f32[8,4,32,128]{3,2,1,0:T(8,128)S(1)}) custom-call(s32[4,8,128]{2,1,0:T(8,128)} %bits_hbm.1, s32[4,8,128]{2,1,0:T(8,128)} %dis_hbm.1), custom_call_target="tpu_custom_call" | custom-call | tf_op jit(solution)/shard_map/pallas_call | solution.py:488
  33.8 1.0 %shard_map.50 = (f32[3,8]{1,0:T(4,128)}, f32[8,4,32,128]{3,2,1,0:T(8,128)}, f32[8,4,32,128]{3,2,1,0:T(8,128)}) custom-call(f32[3,8]{1,0:T(4,128)S(1)} %get-tuple-element.6.mom, f32[8,4,32,128]{3,2,1,0:T(8,128)S(1)} %get-tuple-element.7.prev, f32[8,4,32,128]{3,2,1,0:T(8,128)S(1)} %get-tuple-element.8.cur), custom_call_target="tpu_custom_call" | custom-call | tf_op jit(solution)/shard_map/pallas_call | solution.py:508

commit v4 on v3

--- a/solution.py
+++ b/solution.py
@@ -332,8 +332,8 @@
 
         lax.fori_loop(0, 8 // group, body, 0)
 
-    probes(pass_a1, 4)
-    probes(pass_a2, 4)
+    probes(pass_a1, 8)
+    probes(pass_a2, 8)
 
     mine = jnp.zeros((8, 128), F32)
     for m in range(3):
@@ -434,18 +434,8 @@
             line_copy(k, 0).start()
         for k in range(1, 8):
             line_copy(k, 1).start()
-        for k in range(1, 8):
-            line_copy(k, 1).wait_recv()
         GL[pl.ds(gx, 1), :] = S[1, 0:1, :]
 
-    @pl.when(core == 0)
-    def _():
-        for k in range(8):
-            line_copy(k, 0).wait_recv()
-
-    total = sum_rows(GL[...]) * (1.0 / NSITES)
-    out = jnp.where(r0, total, jnp.where(row == 1, roll(total, 120, 1), roll(total, 112, 1)))
-    mom[...] = out[:3, :8]
     for cp in halo:
         cp.wait_send()
     for k in range(1, 32):
@@ -454,6 +444,17 @@
     @pl.when(core == 0)
     def _():
         plane_copy(0).wait_send()
+        for k in range(8):
+            line_copy(k, 0).wait_recv()
+
+    @pl.when(core == 1)
+    def _():
+        for k in range(1, 8):
+            line_copy(k, 1).wait_recv()
+
+    total = sum_rows(GL[...]) * (1.0 / NSITES)
+    out = jnp.where(r0, total, jnp.where(row == 1, roll(total, 120, 1), roll(total, 112, 1)))
+    mom[...] = out[:3, :8]
 
     @pl.when(core == 1)
     def _():

time: 35 us -> 34.5 us (0.986)
  Pallas kernels: 34.1 us -> 33.7 us
    pallas_call x1, Pallas kernels: 33.1 us -> 32.7 us  [per_device(): pl.pallas_call(kernel, out_shape=shapes, in_specs=[pl.BlockSpec(memory_sp...]
where the time goes in v4:
time: 34.5 us; the launch traced here: 34.3 us
  Pallas kernels  33.7 us (98%)
  between operations  0.64 us (2%)
    pallas_call x1, Pallas kernels, per_device(): pl.pallas_call(kernel, out_shape=shapes, in_specs=[pl.BlockSpec(memory_sp...  32.7 us
    pallas_call x1, Pallas kernels, per_device(): pl.pallas_call(write_out, out_shape=shapes, in_specs=[pl.BlockSpec(memory...  1 us

profile of v4, /device:TPU:1, one launch (start us, length us, event | category | flops | bytes accessed | tf_op | source)
XLA Modules:
  0.0 34.3 jit_solution(7783530598906856491)
XLA Ops:
  0.6 32.7 %shard_map.49 = (f32[3,8]{1,0:T(4,128)S(1)}, f32[8,4,32,128]{3,2,1,0:T(8,128)S(1)}, f32[8,4,32,128]{3,2,1,0:T(8,128)S(1)}) custom-call(s32[4,8,128]{2,1,0:T(8,128)} %bits_hbm.1, s32[4,8,128]{2,1,0:T(8,128)} %dis_hbm.1), custom_call_target="tpu_custom_call" | custom-call | tf_op jit(solution)/shard_map/pallas_call | solution.py:489
  33.3 1.0 %shard_map.50 = (f32[3,8]{1,0:T(4,128)}, f32[8,4,32,128]{3,2,1,0:T(8,128)}, f32[8,4,32,128]{3,2,1,0:T(8,128)}) custom-call(f32[3,8]{1,0:T(4,128)S(1)} %get-tuple-element.6.mom, f32[8,4,32,128]{3,2,1,0:T(8,128)S(1)} %get-tuple-element.7.prev, f32[8,4,32,128]{3,2,1,0:T(8,128)S(1)} %get-tuple-element.8.cur), custom_call_target="tpu_custom_call" | custom-call | tf_op jit(solution)/shard_map/pallas_call | solution.py:509

commit v5 on v4

--- a/solution.py
+++ b/solution.py
@@ -127,13 +127,12 @@
         pl.semaphore_wait(barrier, 26 + 31 + 15)
 
 
-    halo = []
-    for i, (dx, dy, dz) in enumerate(DIRS):
-        n = 3 - abs(dy) - abs(dz)
+    def halo_copy(i, d, lo, hi):
+        dx, dy, dz = d
         if dx == 1:
-            xs, xd = slice(7 - n, 7), slice(3 - n, 3)
+            xs, xd = slice(7 - hi, 7 - lo), slice(3 - hi, 3 - lo)
         elif dx == -1:
-            xs, xd = slice(3, 3 + n), slice(7, 7 + n)
+            xs, xd = slice(3 + lo, 3 + hi), slice(7 + lo, 7 + hi)
         else:
             xs, xd = slice(3, 7), slice(3, 7)
         if dz == 1:
@@ -142,26 +141,36 @@
             ws, wd = slice(0, 1), slice(8, 9)
         else:
             ws, wd = slice(0, 8), slice(0, 8)
-        cp = pltpu.make_async_remote_copy(
+        return pltpu.make_async_remote_copy(
             src_ref=E.at[:, 1, xs, ws, :],
             dst_ref=E.at[:, 1 - dy, xd, wd, :],
             send_sem=hs.at[i],
             recv_sem=hr.at[i],
-            device_id=neighbour((dx, dy, dz)),
+            device_id=neighbour(d),
             device_id_type=MESH,
         )
+
+    first, rest = [], []
+    for d in DIRS:
+        depth = 2 - abs(d[1]) - abs(d[2])
+        if d[0] == 0 or depth > 0:
+            first.append((d, halo_copy(len(first), d, 0, depth)))
+    for d in DIRS:
+        depth = 2 - abs(d[1]) - abs(d[2])
+        if d[0] != 0:
+            rest.append((d, halo_copy(len(first) + len(rest), d, depth, depth + 1)))
+    for d, cp in first + rest:
         cp.start()
-        halo.append(cp)
-    for cp, d in zip(halo, DIRS):
+    for d, cp in first:
         if d[2] == 0:
             cp.wait_recv()
 
     def tile(a, t, xi, second):
         return E[a, t, xi + 1, (8 if second else 0) : (16 if second else 8), :]
 
-    def pack_y(a, second):
+    def pack_y(a, second, span):
         out = jnp.zeros((8, 128), I32)
-        for xi in range(8):
+        for xi in span:
             left, own, right = (tile(a, t, xi, second) for t in range(3))
             m1 = jnp.where(lane >= 64, left, own)
             m2 = jnp.where(lane >= 64, own, right)
@@ -202,47 +211,41 @@
         x = a ^ b
         return x ^ c, (a & b) | (c & x)
 
-    for xi in range(8):
+    def main_near(xi):
         dis = tile(1, 1, xi, False)
         for j in range(4):
             EPM[xi, j], EMM[xi, j] = weights(dis, 8 * j)
-            if 1 <= xi <= 6:
-                E2M[xi, j] = slope(dis, 8 * j)
         ym, yp = sides(0, xi, False)
         LAT[xi, 0], LAT[xi, 1] = half_count(tile(0, 1, xi + 1, False), tile(0, 1, xi - 1, False), yp)
         LAT[xi, 2] = ym
-    yw, yd = pack_y(0, False), pack_y(1, False)
-    for j in range(4):
-        EPY[j], EMY[j] = weights(yd, 8 * j)
-        E2Y[j] = slope(yd, 8 * j)
-    for cp, d in zip(halo, DIRS):
-        if d[2] != 0:
-            cp.wait_recv()
-
-    for xi in range(8):
+
+    def main_slope(xi):
+        for j in range(4):
+            E2M[xi, j] = slope(tile(1, 1, xi, False), 8 * j)
+
+    def main_words(xi):
         main, second = tile(0, 1, xi, False), tile(0, 1, xi, True)
-        up, down = up_down(main, second)
-        zp, zm = z_words(main, up, down)
+        zp, zm = z_words(main, *up_down(main, second))
         planes = add_counts(LAT[xi, 0], LAT[xi, 1], *half_count(LAT[xi, 2], zp, zm))
         for j in range(4):
             NM[xi, j] = nibbles(planes, main, j)
-        if 1 <= xi <= 6:
-            up, down = up_down(second, main)
-            zp, zm = z_words(second, up, down)
-            ym, yp = sides(0, xi, True)
-            dis = tile(1, 1, xi, True)
-            planes = add_counts(
-                *half_count(tile(0, 1, xi + 1, True), tile(0, 1, xi - 1, True), yp),
-                *half_count(ym, zp, zm),
-            )
+
+    def edge_words(xi, shallow, deep):
+        main, second = tile(0, 1, xi, False), tile(0, 1, xi, True)
+        zp, zm = z_words(second, *up_down(second, main))
+        ym, yp = sides(0, xi, True)
+        dis = tile(1, 1, xi, True)
+        planes = add_counts(
+            *half_count(tile(0, 1, xi + 1, True), tile(0, 1, xi - 1, True), yp),
+            *half_count(ym, zp, zm),
+        )
+        if shallow:
             NZ1[xi - 1] = nibbles(planes, second, zshift(1, 1))
             EPZ1[xi - 1], EMZ1[xi - 1] = weights(dis, zshift(1, 8))
-            if 2 <= xi <= 5:
-                E2Z[xi - 2] = slope(dis, zshift(1, 8))
-                NZ2[xi - 2] = nibbles(planes, second, zshift(2, 1))
-                EPZ2[xi - 2], EMZ2[xi - 2] = weights(dis, zshift(2, 8))
-
-    yw2, yd2 = pack_y(0, True), pack_y(1, True)
+        if deep:
+            E2Z[xi - 2] = slope(dis, zshift(1, 8))
+            NZ2[xi - 2] = nibbles(planes, second, zshift(2, 1))
+            EPZ2[xi - 2], EMZ2[xi - 2] = weights(dis, zshift(2, 8))
 
     def y_planes(word, up, down):
         zp, zm = z_words(word, up, down)
@@ -251,12 +254,31 @@
             *half_count(roll(word, 112, 1), zp, zm),
         )
 
-    planes = y_planes(yw, *up_down(yw, yw2))
-    for j in range(4):
-        NY[j] = nibbles(planes, yw, j)
-    planes = y_planes(yw2, *up_down(yw2, yw))
-    NY2[...] = nibbles(planes, yw2, zshift(1, 1))
-    EPY2[...], EMY2[...] = weights(yd2, zshift(1, 8))
+    def y_words(yw, yw2):
+        planes = y_planes(yw, *up_down(yw, yw2))
+        for j in range(4):
+            NY[j] = nibbles(planes, yw, j)
+
+    def y_weights(yd):
+        for j in range(4):
+            EPY[j], EMY[j] = weights(yd, 8 * j)
+
+    for xi in range(1, 7):
+        main_near(xi)
+    for xi in range(2, 6):
+        main_slope(xi)
+    yw = pack_y(0, False, range(1, 7))
+    y_weights(pack_y(1, False, range(1, 7)))
+
+    for d, cp in first:
+        if d[2] != 0:
+            cp.wait_recv()
+
+    for xi in range(1, 7):
+        main_words(xi)
+    for xi in range(2, 6):
+        edge_words(xi, True, False)
+    y_words(yw, pack_y(0, True, range(2, 6)))
 
     col = lane & 15
 
@@ -287,21 +309,38 @@
         c, s = around(lambda x, k: V1M[r, x, k], lambda x: V1Z1[r, x - 1], V1YI[r, j], xi, j)
         return c, (E2M[xi, j] * c - C2 * s) * C2 - sg
 
-    def pass_a1(r):
-        sh = 28 - 4 * r
-        for xi in range(8):
-            for j in range(4):
-                V1M[r, xi, j] = first_order(NM[xi, j], EPM[xi, j], EMM[xi, j], sh)
-                if 2 <= xi <= 5:
-                    SG[r, xi - 2, j] = sign(NM[xi, j], sh)
-        for xi in range(6):
-            V1Z1[r, xi] = first_order(NZ1[xi], EPZ1[xi], EMZ1[xi], sh)
-        for xi in range(4):
-            V1Z2[r, xi] = first_order(NZ2[xi], EPZ2[xi], EMZ2[xi], sh)
+    def main_first(r, xi, sh):
+        for j in range(4):
+            V1M[r, xi, j] = first_order(NM[xi, j], EPM[xi, j], EMM[xi, j], sh)
+
+    def edge_first(r, xi, sh):
+        V1Z1[r, xi - 1] = first_order(NZ1[xi - 1], EPZ1[xi - 1], EMZ1[xi - 1], sh)
+
+    def y_first(r, sh):
         for j in range(4):
             y = first_order(NY[j], EPY[j], EMY[j], sh)
             V1Y[r, j] = y
             V1YI[r, j] = inner(y)
+
+    def pass_a1(r):
+        sh = 28 - 4 * r
+        for xi in range(1, 7):
+            main_first(r, xi, sh)
+        for xi in range(2, 6):
+            edge_first(r, xi, sh)
+            for j in range(4):
+                SG[r, xi - 2, j] = sign(NM[xi, j], sh)
+        y_first(r, sh)
+
+    def pass_a3(r):
+        sh = 28 - 4 * r
+        for xi in (0, 7):
+            main_first(r, xi, sh)
+        for xi in (1, 6):
+            edge_first(r, xi, sh)
+        for xi in range(4):
+            V1Z2[r, xi] = first_order(NZ2[xi], EPZ2[xi], EMZ2[xi], sh)
+        y_first(r, sh)
         y = first_order(NY2[...], EPY2[...], EMY2[...], sh)
         V1Y2[r] = y
         V1Y2I[r] = inner(y)
@@ -388,6 +427,26 @@
         plane_copy(0).start()
 
 
+    for d, cp in rest:
+        cp.wait_recv()
+    for xi in (0, 7):
+        main_near(xi)
+        main_words(xi)
+    for xi in (1, 6):
+        main_slope(xi)
+        edge_words(xi, True, False)
+    for xi in range(2, 6):
+        edge_words(xi, False, True)
+    yw, yw2 = pack_y(0, False, range(8)), pack_y(0, True, range(8))
+    yd, yd2 = pack_y(1, False, range(8)), pack_y(1, True, range(8))
+    y_words(yw, yw2)
+    y_weights(yd)
+    for j in range(4):
+        E2Y[j] = slope(yd, 8 * j)
+    NY2[...] = nibbles(y_planes(yw2, *up_down(yw2, yw)), yw2, zshift(1, 1))
+    EPY2[...], EMY2[...] = weights(yd2, zshift(1, 8))
+    probes(pass_a3, 2)
+
     def pass_b(r):
         sh = 28 - 4 * r
         for xi, slot2 in ((1, 0), (6, 5)):
@@ -436,7 +495,7 @@
             line_copy(k, 1).start()
         GL[pl.ds(gx, 1), :] = S[1, 0:1, :]
 
-    for cp in halo:
+    for _, cp in first + rest:
         cp.wait_send()
     for k in range(1, 32):
         plane_copy(k).wait_send()
@@ -500,7 +559,7 @@
             vm(8, 8, 4), vm(8, 6), vm(8, 4), vm(8, 4), vm(8, 4), vm(8), vm(8),
             vm(8, 6, 4), vm(8, 4), vm(8, 4),
             vm(3), vm(2), pltpu.VMEM((64, 128), F32), vm(),
-            dma((2,)), dma((26,)), dma((26,)), dma((32,)), dma((64,)), dma((16,)), dma((16,)),
+            dma((2,)), dma((38,)), dma((38,)), dma((32,)), dma((64,)), dma((16,)), dma((16,)),
         ],
         compiler_params=pltpu.CompilerParams(
             collective_id=0, has_side_effects=True, vmem_limit_bytes=24 * 1024 * 1024

time: 34.5 us -> 34.3 us (level)
  no operation moved by 1% of the time
where the time goes in v5:
time: 34.3 us; the launch traced here: 34.1 us
  Pallas kernels  33.4 us (97%)
  between operations  0.64 us (2%)
    pallas_call x1, Pallas kernels, per_device(): pl.pallas_call(kernel, out_shape=shapes, in_specs=[pl.BlockSpec(memory_sp...  32.4 us
    pallas_call x1, Pallas kernels, per_device(): pl.pallas_call(write_out, out_shape=shapes, in_specs=[pl.BlockSpec(memory...  1 us

profile of v5, /device:TPU:1, one launch (start us, length us, event | category | flops | bytes accessed | tf_op | source)
XLA Modules:
  0.0 34.1 jit_solution(208803748581309720)
XLA Ops:
  0.6 32.4 %shard_map.49 = (f32[3,8]{1,0:T(4,128)S(1)}, f32[8,4,32,128]{3,2,1,0:T(8,128)S(1)}, f32[8,4,32,128]{3,2,1,0:T(8,128)S(1)}) custom-call(s32[4,8,128]{2,1,0:T(8,128)} %bits_hbm.1, s32[4,8,128]{2,1,0:T(8,128)} %dis_hbm.1), custom_call_target="tpu_custom_call" | custom-call | tf_op jit(solution)/shard_map/pallas_call | solution.py:548
  33.1 1.0 %shard_map.50 = (f32[3,8]{1,0:T(4,128)}, f32[8,4,32,128]{3,2,1,0:T(8,128)}, f32[8,4,32,128]{3,2,1,0:T(8,128)}) custom-call(f32[3,8]{1,0:T(4,128)S(1)} %get-tuple-element.6.mom, f32[8,4,32,128]{3,2,1,0:T(8,128)S(1)} %get-tuple-element.7.prev, f32[8,4,32,128]{3,2,1,0:T(8,128)S(1)} %get-tuple-element.8.cur), custom_call_target="tpu_custom_call" | custom-call | tf_op jit(solution)/shard_map/pallas_call | solution.py:568

commit v6 on v5

--- a/solution.py
+++ b/solution.py
@@ -51,7 +51,7 @@
 
 def kernel(
     bits_hbm, dis_hbm, mom, prev, cur,
-    E, LAT, SG, NM, NZ1, NZ2, NY, NY2,
+    E, LAT, NM, NZ1, NZ2, NY, NY2,
     EPM, EMM, E2M, EPZ1, EMZ1, EPZ2, EMZ2, E2Z, EPY, EMY, E2Y, EPY2, EMY2,
     V1M, V1Z1, V1Z2, V1Y, V1YI, V1Y2I, V1Y2, V2M, V2Z, V2YI, ACC, S, GP, GL,
     in_sem, hs, hr, ps, pr, ls, lr,
@@ -324,17 +324,15 @@
 
     def pass_a1(r):
         sh = 28 - 4 * r
-        for xi in range(1, 7):
+        for xi in range(2, 7):
             main_first(r, xi, sh)
         for xi in range(2, 6):
             edge_first(r, xi, sh)
-            for j in range(4):
-                SG[r, xi - 2, j] = sign(NM[xi, j], sh)
         y_first(r, sh)
 
     def pass_a3(r):
         sh = 28 - 4 * r
-        for xi in (0, 7):
+        for xi in (0, 1, 7):
             main_first(r, xi, sh)
         for xi in (1, 6):
             edge_first(r, xi, sh)
@@ -345,23 +343,35 @@
         V1Y2[r] = y
         V1Y2I[r] = inner(y)
 
+    def moments_of(r):
+        sh = 28 - 4 * r
+        own = jnp.zeros((8, 128), F32)
+        square = jnp.zeros((8, 128), F32)
+        onsite = jnp.zeros((8, 128), F32)
+        bonds = jnp.zeros((8, 128), F32)
+        for xi in range(2, 6):
+            for j in range(4):
+                c = V1M[r, xi, j]
+                side = roll(V1YI[r, j], 0 - (16 * xi + 2), 1)
+                above = V1M[r, xi, j + 1] if j < 3 else roll(jnp.where(r0, V1Z1[r, xi - 1], V1M[r, xi, 0]), 7, 0)
+                ahead = V1M[r, xi + 1, j] + jnp.where(l127, side, roll(c, 127, 1)) + above
+                c2 = c * c
+                own = own + jnp.where(top(NM[xi, j], sh) < 0, c, 0.0 - c)
+                square = square + c2
+                onsite = onsite + E2M[xi, j] * c2
+                bonds = bonds + c * ahead
+        m3 = (2.0 * C2 * C2) * (onsite - (2.0 * C2) * bonds) - (3.0 * C2) * own
+        m2 = (2.0 * C2 * C2) * square - float(LOCAL // 1024)
+        for m, acc in enumerate((C2 * own, m2, m3)):
+            ACC[m, pl.ds(r, 1), :] = jnp.sum(acc, axis=0, keepdims=True)
+
     def pass_a2(r):
-        a1 = jnp.zeros((8, 128), F32)
-        a2 = jnp.zeros((8, 128), F32)
-        a3 = jnp.zeros((8, 128), F32)
+        sh = 28 - 4 * r
         for x in range(4):
             for j in range(4):
-                sg = SG[r, x, j]
-                v1, v2 = second_main(r, x + 2, j, sg)
+                v2 = second_main(r, x + 2, j, sign(NM[x + 2, j], sh))[1]
                 V2M[r, x + 1, j] = v2
                 prev[r, x, pl.ds(j, 8, stride=4), :] = v2
-                a1 = a1 + sg * v1
-                a2 = a2 + v1 * v1
-                a3 = a3 + v1 * v2
-        a3 = (2.0 * C2) * a3 - C2 * a1
-        a2 = (2.0 * C2 * C2) * a2 - float(LOCAL // 1024)
-        for m, acc in enumerate((C2 * a1, a2, a3)):
-            ACC[m, pl.ds(r, 1), :] = jnp.sum(acc, axis=0, keepdims=True)
 
     def probes(one, group):
         def body(g, carry):
@@ -372,7 +382,7 @@
         lax.fori_loop(0, 8 // group, body, 0)
 
     probes(pass_a1, 8)
-    probes(pass_a2, 8)
+    probes(moments_of, 8)
 
     mine = jnp.zeros((8, 128), F32)
     for m in range(3):
@@ -446,6 +456,7 @@
     NY2[...] = nibbles(y_planes(yw2, *up_down(yw2, yw)), yw2, zshift(1, 1))
     EPY2[...], EMY2[...] = weights(yd2, zshift(1, 8))
     probes(pass_a3, 2)
+    probes(pass_a2, 4)
 
     def pass_b(r):
         sh = 28 - 4 * r
@@ -552,7 +563,7 @@
         out_specs=(pl.BlockSpec(memory_space=pltpu.VMEM),) * 3,
         scratch_shapes=[
             pltpu.VMEM((2, 3, 10, 16, 128), I32),
-            vm(8, 3, dtype=I32), vm(8, 4, 4), vm(8, 4, dtype=I32), vm(6, dtype=I32), vm(4, dtype=I32), vm(4, dtype=I32), vm(dtype=I32),
+            vm(8, 3, dtype=I32), vm(8, 4, dtype=I32), vm(6, dtype=I32), vm(4, dtype=I32), vm(4, dtype=I32), vm(dtype=I32),
             vm(8, 4), vm(8, 4), vm(8, 4),
             vm(6), vm(6), vm(4), vm(4), vm(4),
             vm(4), vm(4), vm(4), vm(), vm(),

time: 34.3 us -> 34.1 us (level)
  no operation moved by 1% of the time
where the time goes in v6:
time: 34.1 us; the launch traced here: 33.9 us
  Pallas kernels  33.3 us (98%)
  between operations  0.64 us (2%)
    pallas_call x1, Pallas kernels, per_device(): pl.pallas_call(kernel, out_shape=shapes, in_specs=[pl.BlockSpec(memory_sp...  32.3 us
    pallas_call x1, Pallas kernels, per_device(): pl.pallas_call(write_out, out_shape=shapes, in_specs=[pl.BlockSpec(memory...  1 us

profile of v6, /device:TPU:1, one launch (start us, length us, event | category | flops | bytes accessed | tf_op | source)
XLA Modules:
  0.0 33.9 jit_solution(15717146391320211131)
XLA Ops:
  0.6 32.3 %shard_map.49 = (f32[3,8]{1,0:T(4,128)S(1)}, f32[8,4,32,128]{3,2,1,0:T(8,128)S(1)}, f32[8,4,32,128]{3,2,1,0:T(8,128)S(1)}) custom-call(s32[4,8,128]{2,1,0:T(8,128)} %bits_hbm.1, s32[4,8,128]{2,1,0:T(8,128)} %dis_hbm.1), custom_call_target="tpu_custom_call" | custom-call | tf_op jit(solution)/shard_map/pallas_call | solution.py:559
  32.9 1.0 %shard_map.50 = (f32[3,8]{1,0:T(4,128)}, f32[8,4,32,128]{3,2,1,0:T(8,128)}, f32[8,4,32,128]{3,2,1,0:T(8,128)}) custom-call(f32[3,8]{1,0:T(4,128)S(1)} %get-tuple-element.6.mom, f32[8,4,32,128]{3,2,1,0:T(8,128)S(1)} %get-tuple-element.7.prev, f32[8,4,32,128]{3,2,1,0:T(8,128)S(1)} %get-tuple-element.8.cur), custom_call_target="tpu_custom_call" | custom-call | tf_op jit(solution)/shard_map/pallas_call | solution.py:579

commit v7 on v6

--- a/solution.py
+++ b/solution.py
@@ -107,8 +107,6 @@
     def _():
         for k in range(1, 32):
             greet(plane_peer(k, 1))
-        for k in range(32):
-            greet(plane_peer(k, 0))
 
     lane = lax.broadcasted_iota(I32, (8, 128), 1)
     row = lax.broadcasted_iota(I32, (8, 128), 0)
@@ -120,7 +118,7 @@
 
     @pl.when(core == 0)
     def _():
-        pl.semaphore_wait(barrier, 26 + 32)
+        pl.semaphore_wait(barrier, 26)
 
     @pl.when(core == 1)
     def _():
@@ -396,14 +394,12 @@
 
     mine = sum_rows(mine)
 
-    slot = place * 2 + core
-
     def plane_copy(k):
         return pltpu.make_async_remote_copy(
             src_ref=S.at[0, 0:1, :],
-            dst_ref=GP.at[pl.ds(slot, 1), :],
+            dst_ref=GP.at[pl.ds(place, 1), :] if k else GP.at[32:33, :],
             send_sem=ps.at[k],
-            recv_sem=pr.at[(1 - core) * 32 + k],
+            recv_sem=pr.at[k],
             device_id=plane_peer(k, 1),
             device_id_type=MESH,
         )
@@ -418,23 +414,18 @@
             device_id_type=MESH,
         )
 
-    def plane_arrived(q):
-        return pltpu.make_async_remote_copy(
-            src_ref=S.at[0, 0:1, :],
-            dst_ref=GP.at[0:1, :],
-            send_sem=ps.at[0],
-            recv_sem=pr.at[q],
-            device_id=plane_peer(1, 1),
-            device_id_type=MESH,
-        ).wait_recv()
-
     S[0] = mine
-    for k in range(1, 32):
-        plane_copy(k).start()
 
     @pl.when(core == 0)
     def _():
         plane_copy(0).start()
+
+    @pl.when(core == 1)
+    def _():
+        plane_copy(0).wait_recv()
+        S[0] = mine + GP[32:33, :]
+        for k in range(1, 32):
+            plane_copy(k).start()
 
 
     for d, cp in rest:
@@ -494,11 +485,11 @@
 
     @pl.when(core == 1)
     def _():
-        for q in range(1, 64):
-            plane_arrived(q)
+        for k in range(1, 32):
+            plane_copy(k).wait_recv()
         acc = jnp.zeros((8, 128), F32)
-        for q in range(8):
-            acc = acc + jnp.where(row + 8 * q == slot, mine, GP[8 * q : 8 * q + 8, :])
+        for q in range(4):
+            acc = acc + jnp.where(row + 8 * q == place, S[0], GP[8 * q : 8 * q + 8, :])
         S[1] = sum_rows(acc)
         for k in range(8):
             line_copy(k, 0).start()
@@ -508,8 +499,6 @@
 
     for _, cp in first + rest:
         cp.wait_send()
-    for k in range(1, 32):
-        plane_copy(k).wait_send()
 
     @pl.when(core == 0)
     def _():
@@ -519,6 +508,8 @@
 
     @pl.when(core == 1)
     def _():
+        for k in range(1, 32):
+            plane_copy(k).wait_send()
         for k in range(1, 8):
             line_copy(k, 1).wait_recv()
 
@@ -569,8 +560,8 @@
             vm(4), vm(4), vm(4), vm(), vm(),
             vm(8, 8, 4), vm(8, 6), vm(8, 4), vm(8, 4), vm(8, 4), vm(8), vm(8),
             vm(8, 6, 4), vm(8, 4), vm(8, 4),
-            vm(3), vm(2), pltpu.VMEM((64, 128), F32), vm(),
-            dma((2,)), dma((38,)), dma((38,)), dma((32,)), dma((64,)), dma((16,)), dma((16,)),
+            vm(3), vm(2), pltpu.VMEM((40, 128), F32), vm(),
+            dma((2,)), dma((38,)), dma((38,)), dma((32,)), dma((32,)), dma((16,)), dma((16,)),
         ],
         compiler_params=pltpu.CompilerParams(
             collective_id=0, has_side_effects=True, vmem_limit_bytes=24 * 1024 * 1024

time: 34.1 us -> 34.3 us (level)
  no operation moved by 1% of the time
where the time goes in v7:
time: 34.3 us; the launch traced here: 34.1 us
  Pallas kernels  33.4 us (97%)
  between operations  0.64 us (2%)
    pallas_call x1, Pallas kernels, per_device(): pl.pallas_call(kernel, out_shape=shapes, in_specs=[pl.BlockSpec(memory_sp...  32.4 us
    pallas_call x1, Pallas kernels, per_device(): pl.pallas_call(write_out, out_shape=shapes, in_specs=[pl.BlockSpec(memory...  1 us

profile of v7, /device:TPU:1, one launch (start us, length us, event | category | flops | bytes accessed | tf_op | source)
XLA Modules:
  0.0 34.1 jit_solution(10482176303323957555)
XLA Ops:
  0.6 32.4 %shard_map.49 = (f32[3,8]{1,0:T(4,128)S(1)}, f32[8,4,32,128]{3,2,1,0:T(8,128)S(1)}, f32[8,4,32,128]{3,2,1,0:T(8,128)S(1)}) custom-call(s32[4,8,128]{2,1,0:T(8,128)} %bits_hbm.1, s32[4,8,128]{2,1,0:T(8,128)} %dis_hbm.1), custom_call_target="tpu_custom_call" | custom-call | tf_op jit(solution)/shard_map/pallas_call | solution.py:550
  33.1 1.0 %shard_map.50 = (f32[3,8]{1,0:T(4,128)}, f32[8,4,32,128]{3,2,1,0:T(8,128)}, f32[8,4,32,128]{3,2,1,0:T(8,128)}) custom-call(f32[3,8]{1,0:T(4,128)S(1)} %get-tuple-element.6.mom, f32[8,4,32,128]{3,2,1,0:T(8,128)S(1)} %get-tuple-element.7.prev, f32[8,4,32,128]{3,2,1,0:T(8,128)S(1)} %get-tuple-element.8.cur), custom_call_target="tpu_custom_call" | custom-call | tf_op jit(solution)/shard_map/pallas_call | solution.py:570

commit v8 on v6

--- a/solution.py
+++ b/solution.py
@@ -522,9 +522,7 @@
         for k in range(1, 8):
             line_copy(k, 1).wait_recv()
 
-    total = sum_rows(GL[...]) * (1.0 / NSITES)
-    out = jnp.where(r0, total, jnp.where(row == 1, roll(total, 120, 1), roll(total, 112, 1)))
-    mom[...] = out[:3, :8]
+    mom[...] = GL[...]
 
     @pl.when(core == 1)
     def _():
@@ -534,13 +532,18 @@
             line_copy(k, 1).wait_send()
 
 
-def write_out(mom, prev, cur, mom_out, prev_out, cur_out, sems):
+def write_out(rows, prev, cur, mom_out, prev_out, cur_out, mom, sems):
     copies = [
         pltpu.make_async_copy(src, dst, sems.at[i])
         for i, (src, dst) in enumerate(((prev, prev_out), (cur, cur_out), (mom, mom_out)))
     ]
-    for cp in copies:
+    for cp in copies[:2]:
         cp.start()
+    row = lax.broadcasted_iota(I32, (8, 128), 0)
+    total = jnp.broadcast_to(jnp.sum(rows[...], axis=0, keepdims=True), (8, 128)) * (1.0 / NSITES)
+    out = jnp.where(row == 0, total, jnp.where(row == 1, roll(total, 120, 1), roll(total, 112, 1)))
+    mom[...] = out[:3, :8]
+    copies[2].start()
     for cp in copies:
         cp.wait()
 
@@ -558,7 +561,7 @@
     )
     held = pl.pallas_call(
         kernel,
-        out_shape=shapes,
+        out_shape=(jax.ShapeDtypeStruct((8, 128), F32),) + shapes[1:],
         in_specs=[pl.BlockSpec(memory_space=pltpu.HBM)] * 2,
         out_specs=(pl.BlockSpec(memory_space=pltpu.VMEM),) * 3,
         scratch_shapes=[
@@ -581,7 +584,7 @@
         out_shape=shapes,
         in_specs=[pl.BlockSpec(memory_space=pltpu.VMEM)] * 3,
         out_specs=(pl.BlockSpec(memory_space=pltpu.HBM),) * 3,
-        scratch_shapes=[dma((3,))],
+        scratch_shapes=[pltpu.VMEM((3, 8), F32), dma((3,))],
         compiler_params=pltpu.CompilerParams(vmem_limit_bytes=4 * 1024 * 1024),
     )(*held)
 

time: 34.1 us -> 34 us (level)
  no operation moved by 1% of the time
where the time goes in v8:
time: 34 us; the launch traced here: 33.8 us
  Pallas kernels  33.2 us (98%)
  between operations  0.64 us (2%)
    pallas_call x1, Pallas kernels, per_device(): pl.pallas_call(kernel, out_shape=(jax.ShapeDtypeStruct((8, 128), F32),) +...  32.2 us
    pallas_call x1, Pallas kernels, per_device(): pl.pallas_call(write_out, out_shape=shapes, in_specs=[pl.BlockSpec(memory...  1 us

profile of v8, /device:TPU:1, one launch (start us, length us, event | category | flops | bytes accessed | tf_op | source)
XLA Modules:
  0.0 33.8 jit_solution(6039438779631304597)
XLA Ops:
  0.6 32.2 %shard_map.49 = (f32[8,128]{1,0:T(8,128)S(1)}, f32[8,4,32,128]{3,2,1,0:T(8,128)S(1)}, f32[8,4,32,128]{3,2,1,0:T(8,128)S(1)}) custom-call(s32[4,8,128]{2,1,0:T(8,128)} %bits_hbm.1, s32[4,8,128]{2,1,0:T(8,128)} %dis_hbm.1), custom_call_target="tpu_custom_call" | custom-call | tf_op jit(solution)/shard_map/pallas_call | solution.py:562
  32.8 1.0 %shard_map.50 = (f32[3,8]{1,0:T(4,128)}, f32[8,4,32,128]{3,2,1,0:T(8,128)}, f32[8,4,32,128]{3,2,1,0:T(8,128)}) custom-call(f32[8,128]{1,0:T(8,128)S(1)} %get-tuple-element.6.rows, f32[8,4,32,128]{3,2,1,0:T(8,128)S(1)} %get-tuple-element.7.prev, f32[8,4,32,128]{3,2,1,0:T(8,128)S(1)} %get-tuple-element.8.cur), custom_call_target="tpu_custom_call" | custom-call | tf_op jit(solution)/shard_map/pallas_call | solution.py:582
